TPU v7x, 8 devices: a whole 2x2x1 slice. The times are simulated.
8 devices in a mesh: data: 2 (over z, y), stage: 4 (over x, core).
Axes of the slice: x: 2, y: 2, z: 1, core: 2. Of those that a mesh axis runs over, the one named last changes fastest.
Arguments:
- x_init: float32 [64, 64, 64], P('data'), parts along dimension 0
- h_warm: bfloat16 [3, 64, 64, 1024], P(None, 'data'), parts along dimension 1
- w_lat: bfloat16 [4, 64, 1024], P('stage')
- w_qkv: bfloat16 [4, 1024, 3072], P('stage')
- w_o: bfloat16 [4, 16, 64, 1024], P('stage')
- w_up: bfloat16 [4, 1024, 4096], P('stage')
- w_down: bfloat16 [4, 4096, 1024], P('stage')
- w_out: bfloat16 [1024, 64], replicated
- ada_mods: float32 [4, 4, 6, 1024], P(None, 'stage')
- alpha_coef: float32 [4], replicated
- beta_coef: float32 [4], replicated
Outputs:
- output 1: float32 [64, 64, 64], P('data'), parts along dimension 0
- output 2: bfloat16 [4, 64, 64, 1024], P('stage', 'data'), parts along dimension 1
There are 2 independent parts. A program takes and returns all parts, laid end to end along the dimension named above; an argument that names none is the same for every part.
All inputs are finite; a program needn't handle non-finite values.
Results may differ from a plain program's by a relative error of at most 0.02.
Values are sent between devices in bfloat16 or wider.
A program may use at most 1 GiB of HBM per device.

v0:
```python
import jax
import jax.numpy as jnp
from jax import lax
from jax.sharding import PartitionSpec as P


def layer_norm(h_cur):
    row_mean = jnp.mean(h_cur, axis=-1, keepdims=True)
    centered = h_cur - row_mean
    row_var = jnp.mean(centered * centered, axis=-1, keepdims=True)
    return centered * lax.rsqrt(row_var + 1e-6)


def value_a9(h_cur, w_qkv, w_o, w_up, w_down, mod_vec):
    batch_size, tokens = h_cur.shape[0], h_cur.shape[1]
    num_heads, head_dim = w_o.shape[0], w_o.shape[1]
    u_attn = (layer_norm(h_cur) * (1.0 + mod_vec[1]) + mod_vec[0]).astype(jnp.bfloat16)
    qkv_proj = jnp.einsum('bnd,de->bne', u_attn, w_qkv, preferred_element_type=jnp.float32).astype(jnp.bfloat16)
    qkv_proj = qkv_proj.reshape(batch_size, tokens, 3, num_heads, head_dim)
    scores = jnp.einsum('bqhd,bkhd->bhqk', qkv_proj[:, :, 0], qkv_proj[:, :, 1], preferred_element_type=jnp.float32) * head_dim ** -0.5
    attn_probs = jax.nn.softmax(scores, axis=-1).astype(jnp.bfloat16)
    attn_out = jnp.einsum('bhqk,bkhd->bqhd', attn_probs, qkv_proj[:, :, 2], preferred_element_type=jnp.float32).astype(jnp.bfloat16)
    h_cur = h_cur + mod_vec[2] * jnp.einsum('bqhd,hde->bqe', attn_out, w_o, preferred_element_type=jnp.float32)
    u_mlp = (layer_norm(h_cur) * (1.0 + mod_vec[4]) + mod_vec[3]).astype(jnp.bfloat16)
    hidden = jax.nn.gelu(jnp.einsum('bnd,df->bnf', u_mlp, w_up, preferred_element_type=jnp.float32), approximate=True).astype(jnp.bfloat16)
    return h_cur + mod_vec[5] * jnp.einsum('bnf,fd->bnd', hidden, w_down, preferred_element_type=jnp.float32)


def solution(mesh):
    stages = mesh.shape['stage']
    forward = [(dev_idx, dev_idx + 1) for dev_idx in range(stages - 1)]

    def stage_program(x_init, h_warm, w_lat, w_qkv, w_o, w_up, w_down, w_out, ada_mods, alpha_coef, beta_coef):
        stage_idx = lax.axis_index('stage')
        num_steps = ada_mods.shape[0]
        warm_in = lax.dynamic_index_in_dim(h_warm, jnp.maximum(stage_idx - 1, 0), axis=0, keepdims=False)
        stale_in = jnp.where(stage_idx > 0, warm_in, jnp.zeros_like(warm_in))
        x_cur = x_init
        for step_idx in range(num_steps):
            h_cur = stale_in.astype(jnp.float32) + jnp.einsum('bnc,cd->bnd', x_cur.astype(jnp.bfloat16), w_lat[0], preferred_element_type=jnp.float32)
            for layer_idx in range(w_qkv.shape[0]):
                h_cur = value_a9(h_cur, w_qkv[layer_idx], w_o[layer_idx], w_up[layer_idx], w_down[layer_idx], ada_mods[step_idx, layer_idx])
            stage_out = h_cur.astype(jnp.bfloat16)
            if step_idx < num_steps - 1:
                stale_in = lax.ppermute(stage_out, 'stage', perm=forward)
            eps_pred = jnp.einsum('bnd,dc->bnc', stage_out, w_out, preferred_element_type=jnp.float32)
            x_last = jnp.where(stage_idx == stages - 1, alpha_coef[step_idx] * x_cur + beta_coef[step_idx] * eps_pred, 0.0)
            x_cur = lax.psum(x_last, 'stage')
        return x_cur, stage_out[None]

    return jax.shard_map(stage_program, mesh=mesh,
                         in_specs=(P('data'), P(None, 'data'), P('stage'), P('stage'), P('stage'), P('stage'), P('stage'), P(), P(None, 'stage'), P(), P()),
                         out_specs=(P('data'), P('stage', 'data')), check_vma=False)
```

profile of v0, /device:TPU:1, one launch (start us, length us, event | category | flops | bytes accessed | tf_op | source)
XLA Modules:
  0.0 1015.0 jit_solution(17408388714836405444)
XLA Ops:
  18.6 20.3 %convolution_convert_fusion.3 = bf16[32,64,3072]{2,1,0:T(8,128)(2,1)} fusion(bf16[1,1024,3072]{2,1,0:T(8,128)(2,1)} %param.14, f32[32,64,1024]{2,1,0:T(8,128)} %copy-done.1, f32[1024]{0:T(1024)S(1)} %bitcast.249, f32[1024]{0:T(1024)S(1)} %bitcast.250, f32[32,64]{1,0:T(8,128)S(1)} %add_rsqrt_fusion.7, f32[32,64]{1,0:T(8,128)S(1)} %broadcast_multiply_fusion.7), kind=kOutput, calls=%fused_computation.151 | convolution fusion | flops 12901679104 | bytes 27287552 | tf_op jit(solution)/shard_map/bnd,de->bne/dot_general | solution.py:18
  38.9 30.6 %reshape.245 = bf16[32,64,3,16,64]{4,3,2,1,0:T(8,128)(2,1)} reshape(bf16[32,64,3072]{2,1,0:T(8,128)(2,1)} %convolution_convert_fusion.3) | data formatting | bytes 25165824 | tf_op jit(solution)/shard_map/reshape | solution.py:19
  69.5 17.4 %slice_bitcast_fusion.3 = (bf16[32,64,16,64]{3,2,1,0:T(8,128)(2,1)}, bf16[32,64,1,16,64]{4,3,2,1,0:T(8,128)(2,1)}, bf16[32,64,1,16,64]{4,3,2,1,0:T(8,128)(2,1)}) fusion(bf16[32,64,3,16,64]{4,3,2,1,0:T(8,128)(2,1)} %reshape.245), kind=kLoop, calls=%fused_computation.71 | loop fusion | bytes 25165824 | tf_op jit(solution)/shard_map/squeeze | solution.py:22
  100.3 18.5 %fusion.278 = (f32[32,16,64]{2,1,0:T(8,128)S(1)}, f32[32,16,64,64]{2,3,1,0:T(8,128)}) fusion(f32[32,16,64,64]{2,3,1,0:T(8,128)} %fusion.71), kind=kOutput, calls=%fused_computation.270 | output fusion | flops 8388671 | bytes 16908288 | tf_op jit(solution)/shard_map/sub | solution.py:21
  118.8 18.5 %fusion.279 = (f32[32,64]{1,0:T(8,128)S(1)}, f32[32,64,1024]{2,1,0:T(8,128)}) fusion(f32[32,64,1024]{2,1,0:T(8,128)} %copy-done.1, bf16[1,16,64,1024]{3,2,1,0:T(8,128)(2,1)S(1)} %copy-done, f32[32,16,64,64]{2,3,1,0:T(8,128)} %get-tuple-element.49, bf16[32,64,16,64]{3,2,1,0:T(8,128)(2,1)} %get-tuple-element.11, f32[32,16,64]{2,1,0:T(8,128)S(1)} %get-tuple-element.48, ...), kind=kOutput, calls=%fused_computation.271 | convolution fusion | flops 4575983616 | bytes 31600640 | tf_op jit(solution)/shard_map/bqhd,hde->bqe/dot_general | solution.py:23
  141.4 30.9 %fusion.313 = bf16[32,64,4096]{2,1,0:T(8,128)(2,1)} fusion(bf16[1,1024,4096]{2,1,0:T(8,128)(2,1)} %param.16, f32[32,64,1024]{2,1,0:T(8,128)} %get-tuple-element.51, f32[1024]{0:T(1024)S(1)} %bitcast.246, f32[1024]{0:T(1024)S(1)} %bitcast.247, f32[32,64]{1,0:T(8,128)S(1)} %add_rsqrt_fusion.6, f32[32,64]{1,0:T(8,128)S(1)} %broadcast_multiply_fusion.6), kind=kOutput, calls=%fused_computation.15.clone.clone.clone.clone | convolution fusion | flops 17265852416 | bytes 33579008 | tf_op jit(solution)/shard_map/bnd,df->bnf/dot_general | solution.py:25
  172.3 24.8 %add_convert_fusion.9 = bf16[32,64,1024]{2,1,0:T(8,128)(2,1)} fusion(f32[32,64,1024]{2,1,0:T(8,128)} %get-tuple-element.51, f32[1024]{0:T(1024)S(1)} %bitcast.245, bf16[1,4096,1024]{2,1,0:T(8,128)(2,1)} %param.17, bf16[32,64,4096]{2,1,0:T(8,128)(2,1)} %fusion.313), kind=kOutput, calls=%fused_computation.137 | convolution fusion | flops 17186160640 | bytes 37752832 | tf_op jit(solution)/shard_map/bnf,fd->bnd/dot_general | solution.py:26
  208.6 35.3 %all-reduce.5.cloned.1.call-done = f32[32,64,64]{2,1,0:T(8,128)} async-done(((f32[32,64,64]{2,1,0:T(8,128)}), f32[32,64,64]{2,1,0:T(8,128)}) %all-reduce.5.cloned.1.call-update) | async-done | bytes 524304 | tf_op jit(solution)/shard_map/psum | solution.py:48
  243.9 19.9 %collective-permute-done = bf16[32,64,1024]{2,1,0:T(8,128)(2,1)} collective-permute-done((bf16[32,64,1024]{2,1,0:T(8,128)(2,1)}, bf16[32,64,1024]{2,1,0:T(8,128)(2,1)}, u32[]{:S(2)}, u32[]{:S(2)}) %collective-permute-start) | collective-permute-done | bytes 4194336 | tf_op jit(solution)/shard_map/ppermute | solution.py:45
  274.3 21.2 %convolution_convert_fusion.2 = bf16[32,64,3072]{2,1,0:T(8,128)(2,1)} fusion(bf16[1,1024,3072]{2,1,0:T(8,128)(2,1)} %param.14, f32[1024]{0:T(1024)S(1)} %bitcast.243, f32[1024]{0:T(1024)S(1)} %bitcast.244, f32[32,64]{1,0:T(8,128)S(1)} %add_rsqrt_fusion.5, f32[32,64]{1,0:T(8,128)S(1)} %broadcast_multiply_fusion.5, f32[32,64,1024]{2,1,0:T(8,128)} %copy-done.2, ...), kind=kOutput, calls=%fused_computation.150 | convolution fusion | flops 12905873408 | bytes 31481856 | tf_op jit(solution)/shard_map/bnd,de->bne/dot_general | solution.py:18
  295.5 30.6 %reshape.246 = bf16[32,64,3,16,64]{4,3,2,1,0:T(8,128)(2,1)} reshape(bf16[32,64,3072]{2,1,0:T(8,128)(2,1)} %convolution_convert_fusion.2) | data formatting | bytes 25165824 | tf_op jit(solution)/shard_map/reshape | solution.py:19
  356.9 18.5 %fusion.282 = (f32[32,16,64]{2,1,0:T(8,128)S(1)}, f32[32,16,64,64]{2,3,1,0:T(8,128)}) fusion(f32[32,16,64,64]{2,3,1,0:T(8,128)} %fusion.70), kind=kOutput, calls=%fused_computation.272 | output fusion | flops 8388671 | bytes 16908288 | tf_op jit(solution)/shard_map/sub | solution.py:21
  375.4 19.3 %fusion.283 = (f32[32,64]{1,0:T(8,128)S(1)}, f32[32,64,1024]{2,1,0:T(8,128)}) fusion(bf16[1,16,64,1024]{3,2,1,0:T(8,128)(2,1)S(1)} %copy-done, f32[32,16,64,64]{2,3,1,0:T(8,128)} %get-tuple-element.55, bf16[32,64,16,64]{3,2,1,0:T(8,128)(2,1)} %get-tuple-element.8, f32[32,16,64]{2,1,0:T(8,128)S(1)} %get-tuple-element.54, f32[1024]{0:T(1024)S(1)} %bitcast.242, ...), kind=kOutput, calls=%fused_computation.273 | convolution fusion | flops 4580177920 | bytes 35794944 | tf_op jit(solution)/shard_map/bqhd,hde->bqe/dot_general | solution.py:23
  398.8 30.9 %fusion.310 = bf16[32,64,4096]{2,1,0:T(8,128)(2,1)} fusion(bf16[1,1024,4096]{2,1,0:T(8,128)(2,1)} %param.16, f32[32,64,1024]{2,1,0:T(8,128)} %get-tuple-element.57, f32[1024]{0:T(1024)S(1)} %bitcast.240, f32[1024]{0:T(1024)S(1)} %bitcast.241, f32[32,64]{1,0:T(8,128)S(1)} %add_rsqrt_fusion.4, f32[32,64]{1,0:T(8,128)S(1)} %broadcast_multiply_fusion.4), kind=kOutput, calls=%fused_computation.23.clone.clone.clone.clone | convolution fusion | flops 17265852416 | bytes 33579008 | tf_op jit(solution)/shard_map/bnd,df->bnf/dot_general | solution.py:25
  429.7 24.8 %add_convert_fusion.6 = bf16[32,64,1024]{2,1,0:T(8,128)(2,1)} fusion(f32[32,64,1024]{2,1,0:T(8,128)} %get-tuple-element.57, f32[1024]{0:T(1024)S(1)} %bitcast.239, bf16[1,4096,1024]{2,1,0:T(8,128)(2,1)} %param.17, bf16[32,64,4096]{2,1,0:T(8,128)(2,1)} %fusion.310), kind=kOutput, calls=%fused_computation.129 | convolution fusion | flops 17186160640 | bytes 37752832 | tf_op jit(solution)/shard_map/bnf,fd->bnd/dot_general | solution.py:26
  464.6 34.8 %all-reduce.7.cloned.1.call-done = f32[32,64,64]{2,1,0:T(8,128)} async-done(((f32[32,64,64]{2,1,0:T(8,128)}), f32[32,64,64]{2,1,0:T(8,128)}) %all-reduce.7.cloned.1.call-update) | async-done | bytes 524304 | tf_op jit(solution)/shard_map/psum | solution.py:48
  499.5 21.7 %collective-permute-done.1 = bf16[32,64,1024]{2,1,0:T(8,128)(2,1)} collective-permute-done((bf16[32,64,1024]{2,1,0:T(8,128)(2,1)}, bf16[32,64,1024]{2,1,0:T(8,128)(2,1)}, u32[]{:S(2)}, u32[]{:S(2)}) %collective-permute-start.1) | collective-permute-done | bytes 4194336 | tf_op jit(solution)/shard_map/ppermute | solution.py:45
  531.6 21.2 %convolution_convert_fusion.1 = bf16[32,64,3072]{2,1,0:T(8,128)(2,1)} fusion(bf16[1,1024,3072]{2,1,0:T(8,128)(2,1)} %param.14, f32[1024]{0:T(1024)S(1)} %bitcast.237, f32[1024]{0:T(1024)S(1)} %bitcast.238, f32[32,64]{1,0:T(8,128)S(1)} %add_rsqrt_fusion.3, f32[32,64]{1,0:T(8,128)S(1)} %broadcast_multiply_fusion.3, f32[32,64,1024]{2,1,0:T(8,128)} %copy-done.3, ...), kind=kOutput, calls=%fused_computation.149 | convolution fusion | flops 12905873408 | bytes 31481856 | tf_op jit(solution)/shard_map/bnd,de->bne/dot_general | solution.py:18
  552.8 30.6 %reshape.247 = bf16[32,64,3,16,64]{4,3,2,1,0:T(8,128)(2,1)} reshape(bf16[32,64,3072]{2,1,0:T(8,128)(2,1)} %convolution_convert_fusion.1) | data formatting | bytes 25165824 | tf_op jit(solution)/shard_map/reshape | solution.py:19
  614.3 18.5 %fusion.286 = (f32[32,16,64]{2,1,0:T(8,128)S(1)}, f32[32,16,64,64]{2,3,1,0:T(8,128)}) fusion(f32[32,16,64,64]{2,3,1,0:T(8,128)} %fusion.69), kind=kOutput, calls=%fused_computation.274 | output fusion | flops 8388671 | bytes 16908288 | tf_op jit(solution)/shard_map/sub | solution.py:21
  632.7 19.3 %fusion.287 = (f32[32,64]{1,0:T(8,128)S(1)}, f32[32,64,1024]{2,1,0:T(8,128)}) fusion(bf16[1,16,64,1024]{3,2,1,0:T(8,128)(2,1)S(1)} %copy-done, f32[32,16,64,64]{2,3,1,0:T(8,128)} %get-tuple-element.61, bf16[32,64,16,64]{3,2,1,0:T(8,128)(2,1)} %get-tuple-element.5, f32[32,16,64]{2,1,0:T(8,128)S(1)} %get-tuple-element.60, f32[1024]{0:T(1024)S(1)} %bitcast.236, ...), kind=kOutput, calls=%fused_computation.275 | convolution fusion | flops 4580177920 | bytes 35794944 | tf_op jit(solution)/shard_map/bqhd,hde->bqe/dot_general | solution.py:23
  656.2 30.9 %fusion.307 = bf16[32,64,4096]{2,1,0:T(8,128)(2,1)} fusion(bf16[1,1024,4096]{2,1,0:T(8,128)(2,1)} %param.16, f32[32,64,1024]{2,1,0:T(8,128)} %get-tuple-element.63, f32[1024]{0:T(1024)S(1)} %bitcast.234, f32[1024]{0:T(1024)S(1)} %bitcast.235, f32[32,64]{1,0:T(8,128)S(1)} %add_rsqrt_fusion.2, f32[32,64]{1,0:T(8,128)S(1)} %broadcast_multiply_fusion.2), kind=kOutput, calls=%fused_computation.31.clone.clone.clone.clone | convolution fusion | flops 17265852416 | bytes 33579008 | tf_op jit(solution)/shard_map/bnd,df->bnf/dot_general | solution.py:25
  687.1 24.8 %add_convert_fusion.3 = bf16[32,64,1024]{2,1,0:T(8,128)(2,1)} fusion(f32[32,64,1024]{2,1,0:T(8,128)} %get-tuple-element.63, f32[1024]{0:T(1024)S(1)} %bitcast.233, bf16[1,4096,1024]{2,1,0:T(8,128)(2,1)} %param.17, bf16[32,64,4096]{2,1,0:T(8,128)(2,1)} %fusion.307), kind=kOutput, calls=%fused_computation.121 | convolution fusion | flops 17186160640 | bytes 37752832 | tf_op jit(solution)/shard_map/bnf,fd->bnd/dot_general | solution.py:26
  722.0 34.8 %all-reduce.9.cloned.1.call-done = f32[32,64,64]{2,1,0:T(8,128)} async-done(((f32[32,64,64]{2,1,0:T(8,128)}), f32[32,64,64]{2,1,0:T(8,128)}) %all-reduce.9.cloned.1.call-update) | async-done | bytes 524304 | tf_op jit(solution)/shard_map/psum | solution.py:48
  756.9 21.6 %collective-permute-done.2 = bf16[32,64,1024]{2,1,0:T(8,128)(2,1)} collective-permute-done((bf16[32,64,1024]{2,1,0:T(8,128)(2,1)}, bf16[32,64,1024]{2,1,0:T(8,128)(2,1)}, u32[]{:S(2)}, u32[]{:S(2)}) %collective-permute-start.2) | collective-permute-done | bytes 4194336 | tf_op jit(solution)/shard_map/ppermute | solution.py:45
  788.9 21.2 %convolution_convert_fusion = bf16[32,64,3072]{2,1,0:T(8,128)(2,1)} fusion(bf16[1,1024,3072]{2,1,0:T(8,128)(2,1)} %param.14, f32[1024]{0:T(1024)S(1)} %bitcast.231, f32[1024]{0:T(1024)S(1)} %bitcast.232, f32[32,64]{1,0:T(8,128)S(1)} %add_rsqrt_fusion.1, f32[32,64]{1,0:T(8,128)S(1)} %broadcast_multiply_fusion.1, f32[32,64,1024]{2,1,0:T(8,128)} %copy-done.4, ...), kind=kOutput, calls=%fused_computation.148 | convolution fusion | flops 12905873408 | bytes 31481856 | tf_op jit(solution)/shard_map/bnd,de->bne/dot_general | solution.py:18
  810.1 30.6 %reshape.248 = bf16[32,64,3,16,64]{4,3,2,1,0:T(8,128)(2,1)} reshape(bf16[32,64,3072]{2,1,0:T(8,128)(2,1)} %convolution_convert_fusion) | data formatting | bytes 25165824 | tf_op jit(solution)/shard_map/reshape | solution.py:19
  871.6 18.5 %fusion.290 = (f32[32,16,64]{2,1,0:T(8,128)S(1)}, f32[32,16,64,64]{2,3,1,0:T(8,128)}) fusion(f32[32,16,64,64]{2,3,1,0:T(8,128)} %fusion.68), kind=kOutput, calls=%fused_computation.276 | output fusion | flops 8388671 | bytes 16908288 | tf_op jit(solution)/shard_map/sub | solution.py:21
  890.1 19.3 %fusion.291 = (f32[32,64]{1,0:T(8,128)S(1)}, f32[32,64,1024]{2,1,0:T(8,128)}) fusion(bf16[1,16,64,1024]{3,2,1,0:T(8,128)(2,1)S(1)} %copy-done, f32[32,16,64,64]{2,3,1,0:T(8,128)} %get-tuple-element.67, bf16[32,64,16,64]{3,2,1,0:T(8,128)(2,1)} %get-tuple-element.2, f32[32,16,64]{2,1,0:T(8,128)S(1)} %get-tuple-element.66, f32[1024]{0:T(1024)S(1)} %bitcast.230, ...), kind=kOutput, calls=%fused_computation.277 | convolution fusion | flops 4580177920 | bytes 35794944 | tf_op jit(solution)/shard_map/bqhd,hde->bqe/dot_general | solution.py:23
  913.5 30.9 %fusion.304 = bf16[32,64,4096]{2,1,0:T(8,128)(2,1)} fusion(bf16[1,1024,4096]{2,1,0:T(8,128)(2,1)} %param.16, f32[32,64,1024]{2,1,0:T(8,128)} %get-tuple-element.69, f32[1024]{0:T(1024)S(1)} %bitcast.227, f32[1024]{0:T(1024)S(1)} %bitcast.229, f32[32,64]{1,0:T(8,128)S(1)} %add_rsqrt_fusion, f32[32,64]{1,0:T(8,128)S(1)} %broadcast_multiply_fusion), kind=kOutput, calls=%fused_computation.39.clone.clone.clone.clone.1 | convolution fusion | flops 17265852416 | bytes 33579008 | tf_op jit(solution)/shard_map/bnd,df->bnf/dot_general | solution.py:25
  944.4 23.7 %add_convert_fusion = bf16[32,64,1024]{2,1,0:T(8,128)(2,1)S(1)} fusion(f32[32,64,1024]{2,1,0:T(8,128)} %get-tuple-element.69, f32[1024]{0:T(1024)S(1)} %bitcast.228, bf16[1,4096,1024]{2,1,0:T(8,128)(2,1)} %param.17, bf16[32,64,4096]{2,1,0:T(8,128)(2,1)} %fusion.304), kind=kOutput, calls=%fused_computation.113 | convolution fusion | flops 17186160640 | bytes 37752832 | tf_op jit(solution)/shard_map/bnf,fd->bnd/dot_general | solution.py:26
  973.6 32.0 %all-reduce.11.cloned.1.call-done = f32[32,64,64]{2,1,0:T(8,128)} async-done(((f32[32,64,64]{2,1,0:T(8,128)}), f32[32,64,64]{2,1,0:T(8,128)}) %all-reduce.11.cloned.1.call-update) | async-done | bytes 524304 | tf_op jit(solution)/shard_map/psum | solution.py:48
  (131 shorter events, 204.1 us)
Async XLA Ops:
  7.2 111.6 %copy-start = (bf16[1,16,64,1024]{3,2,1,0:T(8,128)(2,1)S(1)}, bf16[1,16,64,1024]{3,2,1,0:T(8,128)(2,1)}, u32[]{:S(2)}) copy-start(bf16[1,16,64,1024]{3,2,1,0:T(8,128)(2,1)} %param.15) | copy-start | bytes 6291460
  7.2 236.7 %all-reduce.5.cloned.1.call-start = ((), (), s32[]{:S(2)}) async-start(), calls=%async_computation | async-start | bytes 2097152 | tf_op jit(solution)/shard_map/psum | solution.py:48
  141.4 30.9 %copy-start.37 = (f32[1,1,1,1024]{3,1,2,0:T(1,128)S(1)}, f32[1,1,1,1024]{3,1,2,0:T(1,128)}, u32[]{:S(2)}) copy-start(f32[1,1,1,1024]{3,1,2,0:T(1,128)} %get-tuple-element.34) | copy-start | bytes 12292
  172.3 29.3 %copy-start.17 = (f32[4]{0:T(128)S(1)}, f32[4]{0:T(128)}, u32[]{:S(2)}) copy-start(f32[4]{0:T(128)} %param.20) | copy-start | bytes 52
  172.3 30.0 %copy-start.18 = (f32[4]{0:T(128)S(1)}, f32[4]{0:T(128)}, u32[]{:S(2)}) copy-start(f32[4]{0:T(128)} %param.21) | copy-start | bytes 52
  172.3 30.6 %copy-start.6 = (f32[32,64,64]{2,1,0:T(8,128)S(1)}, f32[32,64,64]{2,1,0:T(8,128)}, u32[]{:S(2)}) copy-start(f32[32,64,64]{2,1,0:T(8,128)} %param.11) | copy-start | bytes 1572868
  172.3 30.6 %copy-start.13 = (bf16[1024,64]{0,1:T(8,128)(2,1)S(1)}, bf16[1024,64]{0,1:T(8,128)(2,1)}, u32[]{:S(2)}) copy-start(bf16[1024,64]{0,1:T(8,128)(2,1)} %param.18) | copy-start | bytes 393220
  172.3 91.6 %copy-start.10 = (bf16[1,64,1024]{2,1,0:T(8,128)(2,1)S(1)}, bf16[1,64,1024]{2,1,0:T(8,128)(2,1)}, u32[]{:S(2)}) copy-start(bf16[1,64,1024]{2,1,0:T(8,128)(2,1)} %param.13) | copy-start | bytes 393220
  197.1 66.8 %collective-permute-start = (bf16[32,64,1024]{2,1,0:T(8,128)(2,1)}, bf16[32,64,1024]{2,1,0:T(8,128)(2,1)}, u32[]{:S(2)}, u32[]{:S(2)}) collective-permute-start(bf16[32,64,1024]{2,1,0:T(8,128)(2,1)} %add_convert_fusion.9), channel_id=1, source_target_pairs={{0,1},{1,2},{2,3},{4,5},{5,6},{6,7}} | collective-permute-start | bytes 12582920 | tf_op jit(solution)/shard_map/ppermute | solution.py:45
  208.6 290.9 %all-reduce.7.cloned.1.call-start = ((), (), s32[]{:S(2)}) async-start(), calls=%async_computation.1 | async-start | bytes 2097152 | tf_op jit(solution)/shard_map/psum | solution.py:48
  267.7 6.6 copy-start.35
  267.7 6.6 copy-start.36
  356.9 18.5 %copy-start.34 = (f32[1,1,1,1024]{3,1,2,0:T(1,128)S(1)}, f32[1,1,1,1024]{3,1,2,0:T(1,128)}, u32[]{:S(2)}) copy-start(f32[1,1,1,1024]{3,1,2,0:T(1,128)} %get-tuple-element.30) | copy-start | bytes 12292
  398.8 30.9 %copy-start.31 = (f32[1,1,1,1024]{3,1,2,0:T(1,128)S(1)}, f32[1,1,1,1024]{3,1,2,0:T(1,128)}, u32[]{:S(2)}) copy-start(f32[1,1,1,1024]{3,1,2,0:T(1,128)} %get-tuple-element.27) | copy-start | bytes 12292
  429.7 29.2 %copy-start.8 = (f32[32,64,64]{2,1,0:T(8,128)S(1)}, f32[32,64,64]{2,1,0:T(8,128)}, u32[]{:S(2)}) copy-start(f32[32,64,64]{2,1,0:T(8,128)} %all-reduce.5.cloned.1.call-done) | copy-start | bytes 1572868
  429.7 29.2 %copy-start.14 = (bf16[1024,64]{0,1:T(8,128)(2,1)S(1)}, bf16[1024,64]{0,1:T(8,128)(2,1)}, u32[]{:S(2)}) copy-start(bf16[1024,64]{0,1:T(8,128)(2,1)} %param.18) | copy-start | bytes 393220
  429.7 91.4 %copy-start.11 = (bf16[1,64,1024]{2,1,0:T(8,128)(2,1)S(1)}, bf16[1,64,1024]{2,1,0:T(8,128)(2,1)}, u32[]{:S(2)}) copy-start(bf16[1,64,1024]{2,1,0:T(8,128)(2,1)} %param.13) | copy-start | bytes 393220
  454.5 66.7 %collective-permute-start.1 = (bf16[32,64,1024]{2,1,0:T(8,128)(2,1)}, bf16[32,64,1024]{2,1,0:T(8,128)(2,1)}, u32[]{:S(2)}, u32[]{:S(2)}) collective-permute-start(bf16[32,64,1024]{2,1,0:T(8,128)(2,1)} %add_convert_fusion.6), channel_id=1, source_target_pairs={{0,1},{1,2},{2,3},{4,5},{5,6},{6,7}} | collective-permute-start | bytes 12582920 | tf_op jit(solution)/shard_map/ppermute | solution.py:45
  464.6 292.3 %all-reduce.9.cloned.1.call-start = ((), (), s32[]{:S(2)}) async-start(), calls=%async_computation.2 | async-start | bytes 2097152 | tf_op jit(solution)/shard_map/psum | solution.py:48
  614.3 18.5 %copy-start.28 = (f32[1,1,1,1024]{3,1,2,0:T(1,128)S(1)}, f32[1,1,1,1024]{3,1,2,0:T(1,128)}, u32[]{:S(2)}) copy-start(f32[1,1,1,1024]{3,1,2,0:T(1,128)} %get-tuple-element.24) | copy-start | bytes 12292
  656.2 30.9 %copy-start.25 = (f32[1,1,1,1024]{3,1,2,0:T(1,128)S(1)}, f32[1,1,1,1024]{3,1,2,0:T(1,128)}, u32[]{:S(2)}) copy-start(f32[1,1,1,1024]{3,1,2,0:T(1,128)} %get-tuple-element.21) | copy-start | bytes 12292
  687.0 29.2 %copy-start.9 = (f32[32,64,64]{2,1,0:T(8,128)S(1)}, f32[32,64,64]{2,1,0:T(8,128)}, u32[]{:S(2)}) copy-start(f32[32,64,64]{2,1,0:T(8,128)} %all-reduce.7.cloned.1.call-done) | copy-start | bytes 1572868
  687.0 29.2 %copy-start.15 = (bf16[1024,64]{0,1:T(8,128)(2,1)S(1)}, bf16[1024,64]{0,1:T(8,128)(2,1)}, u32[]{:S(2)}) copy-start(bf16[1024,64]{0,1:T(8,128)(2,1)} %param.18) | copy-start | bytes 393220
  687.0 91.4 %copy-start.12 = (bf16[1,64,1024]{2,1,0:T(8,128)(2,1)S(1)}, bf16[1,64,1024]{2,1,0:T(8,128)(2,1)}, u32[]{:S(2)}) copy-start(bf16[1,64,1024]{2,1,0:T(8,128)(2,1)} %param.13) | copy-start | bytes 393220
  711.8 66.7 %collective-permute-start.2 = (bf16[32,64,1024]{2,1,0:T(8,128)(2,1)}, bf16[32,64,1024]{2,1,0:T(8,128)(2,1)}, u32[]{:S(2)}, u32[]{:S(2)}) collective-permute-start(bf16[32,64,1024]{2,1,0:T(8,128)(2,1)} %add_convert_fusion.3), channel_id=1, source_target_pairs={{0,1},{1,2},{2,3},{4,5},{5,6},{6,7}} | collective-permute-start | bytes 12582920 | tf_op jit(solution)/shard_map/ppermute | solution.py:45
  722.0 283.7 %all-reduce.11.cloned.1.call-start = ((), (), s32[]{:S(2)}) async-start(), calls=%async_computation.3 | async-start | bytes 2097152 | tf_op jit(solution)/shard_map/psum | solution.py:48
  782.3 6.6 copy-start.23
  782.3 6.6 copy-start.24
  871.6 18.5 %copy-start.22 = (f32[1,1,1,1024]{3,1,2,0:T(1,128)S(1)}, f32[1,1,1,1024]{3,1,2,0:T(1,128)}, u32[]{:S(2)}) copy-start(f32[1,1,1,1024]{3,1,2,0:T(1,128)} %get-tuple-element.18) | copy-start | bytes 12292
  913.5 30.9 %copy-start.20 = (f32[1,1,1,1024]{3,1,2,0:T(1,128)S(1)}, f32[1,1,1,1024]{3,1,2,0:T(1,128)}, u32[]{:S(2)}) copy-start(f32[1,1,1,1024]{3,1,2,0:T(1,128)} %get-tuple-element.15) | copy-start | bytes 12292
  944.4 25.7 %copy-start.7 = (f32[32,64,64]{2,1,0:T(8,128)S(1)}, f32[32,64,64]{2,1,0:T(8,128)}, u32[]{:S(2)}) copy-start(f32[32,64,64]{2,1,0:T(8,128)} %all-reduce.9.cloned.1.call-done) | copy-start | bytes 1572868
  944.4 25.7 %copy-start.16 = (bf16[1024,64]{0,1:T(8,128)(2,1)S(1)}, bf16[1024,64]{0,1:T(8,128)(2,1)}, u32[]{:S(2)}) copy-start(bf16[1024,64]{0,1:T(8,128)(2,1)} %param.18) | copy-start | bytes 393220
  (13 other events, 52.5 us)
Sparse Core Ops, SparseCore 0:
  208.7 35.2 all-reduce.4
  464.7 34.7 all-reduce.6
  722.1 34.7 all-reduce.8
  973.7 31.8 all-reduce.10
where the time goes:
time: 1030 us; the launch traced here: 1010 us
  matrix products  471 us (46%)
  local copies, waits for them, and re-layouts  211 us (20%)
  waiting for transfers between devices  200 us (19%)
  other arithmetic  104 us (10%)
  between operations  14.9 us (1%)
  starting transfers between devices  13.5 us (1%)
    psum x4, waiting for transfers between devices, stage_program(): x_cur = lax.psum(x_last, 'stage')  137 us
    dot_general x4, matrix products, value_a9(): jnp.einsum('bnd,df->bnf', u_mlp, w_up, preferred_element_type=jnp.float32)  123 us
    reshape x4, local copies, waits for them, and re-layouts, value_a9(): qkv_proj = qkv_proj.reshape(batch_size, tokens, 3, num_heads, head_dim)  123 us
    dot_general x4, matrix products, value_a9(): jnp.einsum('bnf,fd->bnd', hidden, w_down, preferred_element_type=jnp.floa...  98 us
    dot_general x4, matrix products, value_a9(): jnp.einsum('bnd,de->bne', u_attn, w_qkv, preferred_element_type=jnp.float32)  83.9 us
    dot_general x4, matrix products, value_a9(): jnp.einsum('bqhd,hde->bqe', attn_out, w_o, preferred_element_type=jnp.flo...  76.6 us
    sub x4, other arithmetic, value_a9(): attn_probs = jax.nn.softmax(scores, axis=-1).astype(jnp.bfloat16)  73.8 us
    squeeze x4, local copies, waits for them, and re-layouts, value_a9(): qkv_proj[:, :, 2]  69.5 us
  transfers between devices with their start and end apart: 7, of which 7 were waited for; matrix products, arithmetic and copies ran while one was open for 2% of the time, Pallas kernels for 0%

commit v1 on v0

v1 whole, which is shorter than its diff:
```python
import functools

import jax
import jax.numpy as jnp
from jax import lax
from jax.experimental import pallas as pl
from jax.experimental.pallas import tpu as pltpu
from jax.sharding import PartitionSpec as P

F32, BF16 = jnp.float32, jnp.bfloat16
MESH = pl.DeviceIdType.MESH
D, HEADS, HEAD, TOK, CH, FF = 1024, 16, 64, 64, 64, 4096
ROWS = 256
RB = 16
STAGES = 4
INV_D = 1.0 / D
GC0 = 0.7978845608028654
GC1 = GC0 * 0.044715


def dot(a, b):
    return jnp.dot(a, b, preferred_element_type=F32)


def dot_t(a, b):
    return lax.dot_general(a, b, (((1,), (1,)), ((), ())), preferred_element_type=F32)


def merge(first, second):
    total_a = sum(w for w, _ in first)
    total_b = sum(w for w, _ in second)
    ia = ib = 0
    done_a = done_b = 0.0
    while ia < len(first) or ib < len(second):
        take_a = ib >= len(second) or (ia < len(first) and done_a / total_a <= done_b / total_b)
        if take_a:
            w, piece = first[ia]
            ia, done_a = ia + 1, done_a + w
        else:
            w, piece = second[ib]
            ib, done_b = ib + 1, done_b + w
        piece()


def kernel(steps, chunks,
           x_hbm, warm_hbm, lat_hbm, qkv_hbm, o_hbm, up_hbm, down_hbm, out_hbm, mods_hbm, alpha, beta,
           xout_hbm, hlast_hbm,
           wlat, wk, wqvt, wo, wup, wdown, wout, wtmp, mods,
           buf, xb, xf, ebuf,
           h_a, h_b, u_a, u_b, k_s, qv_s, o_s, hid,
           w_sem, warm_sem, st_send, st_recv, x_send, x_recv, xo_send, xo_recv, xo_loc, hl_sem):
    st = lax.axis_index('stage')
    last = STAGES - 1
    total = steps * chunks

    loads = [
        pltpu.make_async_copy(qkv_hbm.at[:, pl.ds(0, D)], wtmp.at[0], w_sem.at[0]),
        pltpu.make_async_copy(qkv_hbm.at[:, pl.ds(2 * D, D)], wtmp.at[1], w_sem.at[1]),
        pltpu.make_async_copy(x_hbm, xf, w_sem.at[2]),
        pltpu.make_async_copy(mods_hbm, mods, w_sem.at[3]),
        pltpu.make_async_copy(lat_hbm, wlat, w_sem.at[4]),
        pltpu.make_async_copy(qkv_hbm.at[:, pl.ds(D, D)], wk, w_sem.at[5]),
        pltpu.make_async_copy(o_hbm, wo, w_sem.at[6]),
        pltpu.make_async_copy(up_hbm, wup, w_sem.at[7]),
        pltpu.make_async_copy(down_hbm, wdown, w_sem.at[8]),
        pltpu.make_async_copy(out_hbm, wout, w_sem.at[9]),
    ]
    warm_stage = jnp.maximum(st - 1, 0)

    def warm_copy(c):
        return pltpu.make_async_copy(warm_hbm.at[warm_stage, c], buf.at[c], warm_sem.at[c])

    for ld in loads[:5]:
        ld.start()
    warm_copy(0).start()
    for ld in loads[5:]:
        ld.start()
    for c in range(1, chunks):
        warm_copy(c).start()

    barrier = pltpu.get_barrier_semaphore()
    for k in range(1, STAGES):
        pl.semaphore_signal(barrier, inc=1, device_id={'stage': lax.rem(st + k, STAGES)}, device_id_type=MESH)
    pl.semaphore_wait(barrier, STAGES - 1)

    def stale_copy(k):
        nxt = jnp.minimum(st + 1, last)
        return pltpu.make_async_remote_copy(
            src_ref=buf.at[k], dst_ref=buf.at[k + chunks], send_sem=st_send.at[k], recv_sem=st_recv.at[k],
            device_id={'stage': nxt}, device_id_type=MESH)

    def latent_copy(k, dst):
        return pltpu.make_async_remote_copy(
            src_ref=xb.at[k + chunks], dst_ref=xb.at[k + chunks], send_sem=x_send.at[dst, k], recv_sem=x_recv.at[k],
            device_id={'stage': dst}, device_id_type=MESH)

    def xout_copy(c, dst):
        return pltpu.make_async_remote_copy(
            src_ref=xf.at[c], dst_ref=xout_hbm.at[c], send_sem=xo_send.at[dst, c], recv_sem=xo_recv.at[c],
            device_id={'stage': dst}, device_id_type=MESH)

    def hlast_copy(c):
        return pltpu.make_async_copy(buf.at[(steps - 1) * chunks + c], hlast_hbm.at[c], hl_sem.at[c])

    def wait_inputs(k):
        @pl.when(k < chunks)
        def _():
            warm_copy(k).wait()

        @pl.when(jnp.logical_and(k >= chunks, st > 0))
        def _():
            stale_copy(k - chunks).wait_recv()

        @pl.when(jnp.logical_and(k >= chunks, st < last))
        def _():
            latent_copy(k - chunks, 0).wait_recv()

    def send_stage(k):
        @pl.when(jnp.logical_and(k < total - chunks, st < last))
        def _():
            stale_copy(k).start()

        @pl.when(k >= total - chunks)
        def _():
            hlast_copy(k - (total - chunks)).start()

    def finish_latent(k):
        step, c = lax.div(k, chunks), lax.rem(k, chunks)

        @pl.when(st == last)
        def _():
            x_new = alpha[step] * xf[c] + beta[step] * ebuf[...]
            xf[c] = x_new

            @pl.when(step < steps - 1)
            def _():
                xb[k + chunks] = x_new.astype(BF16)
                for dst in range(last):
                    latent_copy(k, dst).start()

            @pl.when(step == steps - 1)
            def _():
                for dst in range(last):
                    xout_copy(c, dst).start()
                pltpu.make_async_copy(xf.at[c], xout_hbm.at[c], xo_loc.at[c]).start()

    lane = lax.broadcasted_iota(jnp.int32, (HEAD, 4 * TOK), 1)
    left = lax.rem(lane, 2 * TOK) < TOK
    zero_q = jnp.zeros((HEAD, 2 * TOK), BF16)

    def norm(h, scale, shift):
        mean = jnp.sum(h, axis=-1, keepdims=True) * INV_D
        cen = h - mean
        var = jnp.sum(cen * cen, axis=-1, keepdims=True) * INV_D
        return (cen * lax.rsqrt(var + 1e-6) * (1.0 + scale) + shift).astype(BF16)

    def a_pieces(k):
        step = lax.div(k, chunks)
        pieces = []

        def latent(n):
            cols = pl.ds(n * 256, 256)
            h_a[:, cols] = dot(xb[k], wlat[:, cols])

        def norm1(r):
            rows = pl.ds(r * RB, RB)
            stale = jnp.where(st > 0, buf[k, rows, :].astype(F32), 0.0)
            h = stale + h_a[rows, :]
            h_a[rows, :] = h
            u_a[rows, :] = norm(h, mods[step, 1:2, :], mods[step, 0:1, :])

        def proj_k(n):
            cols = pl.ds(n * 256, 256)
            k_s[:, cols] = dot(u_a[...], wk[:, cols]).astype(BF16)

        def proj_qv(n):
            rows = pl.ds(n * 512, 512)
            qv_s[rows, :] = dot_t(wqvt[rows, :], u_a[...]).astype(BF16)

        def attend(p, hp):
            r0, l0 = hp * 2 * HEAD, p * 2 * TOK
            q0 = qv_s[r0:r0 + HEAD, l0:l0 + 2 * TOK]
            q1 = qv_s[r0 + HEAD:r0 + 2 * HEAD, l0:l0 + 2 * TOK]
            rhs = jnp.concatenate([jnp.concatenate([q0, zero_q], axis=1), jnp.concatenate([zero_q, q1], axis=1)], axis=0)
            both = dot(k_s[l0:l0 + 2 * TOK, r0:r0 + 2 * HEAD], rhs)
            s = jnp.where(left, both[:TOK], both[TOK:])
            e = jnp.exp((s - jnp.max(s, axis=0, keepdims=True)) * (HEAD ** -0.5))
            pr = e * (1.0 / jnp.sum(e, axis=0, keepdims=True))
            p_l = jnp.where(left, pr, 0.0).astype(BF16)
            p_r = jnp.where(left, 0.0, pr).astype(BF16)
            h2 = 2 * TOK
            rhs = jnp.concatenate([
                jnp.concatenate([p_l[:, :h2], zero_q], axis=1), jnp.concatenate([p_r[:, :h2], zero_q], axis=1),
                jnp.concatenate([zero_q, p_l[:, h2:]], axis=1), jnp.concatenate([zero_q, p_r[:, h2:]], axis=1)], axis=0)
            v = jnp.concatenate([qv_s[D + r0:D + r0 + HEAD, l0:l0 + h2], qv_s[D + r0 + HEAD:D + r0 + 2 * HEAD, l0:l0 + h2]], axis=1)
            ot = dot(v, rhs)
            ot = jnp.concatenate([ot[:, :h2], ot[:, h2:]], axis=0)
            o_s[l0:l0 + h2, r0:r0 + 2 * HEAD] = ot.T.astype(BF16)

        def proj_o(n):
            cols = pl.ds(n * 256, 256)
            h_a[:, cols] = h_a[:, cols] + mods[step, 2:3, n * 256:(n + 1) * 256] * dot(o_s[...], wo[:, cols])

        for n in range(4):
            pieces.append((64, functools.partial(latent, n)))
        for r in range(ROWS // RB):
            pieces.append((40, functools.partial(norm1, r)))
        for n in range(4):
            pieces.append((256, functools.partial(proj_k, n)))
        for n in range(4):
            pieces.append((512, functools.partial(proj_qv, n)))
        for p in range(2):
            for hp in range(HEADS // 2):
                pieces.append((150, functools.partial(attend, p, hp)))
        for n in range(4):
            pieces.append((256, functools.partial(proj_o, n)))
        return pieces

    def norm2_pieces(k):
        step = lax.div(k, chunks)

        def norm2(r):
            rows = pl.ds(r * RB, RB)
            h = h_a[rows, :]
            h_b[rows, :] = h
            u_b[rows, :] = norm(h, mods[step, 4:5, :], mods[step, 3:4, :])

        return [(40, functools.partial(norm2, r)) for r in range(ROWS // RB)]

    def b_pieces(k):
        step = lax.div(k, chunks)
        pieces = []

        def up(n):
            cols = pl.ds(n * 256, 256)
            z = dot(u_b[...], wup[:, cols])
            half = 0.5 * z
            t = jnp.tanh(z * (GC0 + GC1 * (z * z)))
            hid[:, cols] = (half + half * t).astype(BF16)

        def down(n):
            cols = pl.ds(n * 256, 256)
            y = dot(hid[...], wdown[:, cols])
            buf[k, :, cols] = (h_b[:, cols] + mods[step, 5:6, n * 256:(n + 1) * 256] * y).astype(BF16)

        for n in range(FF // 256):
            pieces.append((256, functools.partial(up, n)))
        for n in range(4):
            pieces.append((1024, functools.partial(down, n)))
        return pieces

    def noise(k):
        ebuf[...] = dot(buf[k], wout[...])

    loads[0].wait()
    loads[1].wait()

    @pl.loop(0, D // 128)
    def _(ii):
        sl = pl.ds(pl.multiple_of(ii * 128, 128), 128)
        for part in range(2):
            wqvt[part * D:(part + 1) * D, sl] = wtmp[part, sl, :].T

    for ld in loads[2:7]:
        ld.wait()
    for c in range(chunks):
        xb[c] = xf[c].astype(BF16)
    wait_inputs(0)
    for _, piece in a_pieces(0):
        piece()
    for _, piece in norm2_pieces(0):
        piece()
    for ld in loads[7:]:
        ld.wait()

    @pl.loop(0, total - 1)
    def _(i):
        wait_inputs(i + 1)
        noise(jnp.maximum(i - 1, 0))
        merge(a_pieces(i + 1), b_pieces(i))
        for _, piece in norm2_pieces(i + 1):
            piece()
        send_stage(i)

        @pl.when(i > 0)
        def _():
            finish_latent(i - 1)

    noise(total - 2)
    for _, piece in b_pieces(total - 1):
        piece()
    send_stage(total - 1)
    finish_latent(total - 2)
    noise(total - 1)
    finish_latent(total - 1)

    for c in range(chunks):
        hlast_copy(c).wait()

    @pl.when(st < last)
    def _():
        @pl.loop(0, total - chunks)
        def _(k):
            stale_copy(k).wait_send()

        for c in range(chunks):
            xout_copy(c, 0).wait_recv()

    @pl.when(st == last)
    def _():
        @pl.loop(0, total - chunks)
        def _(k):
            for dst in range(last):
                latent_copy(k, dst).wait_send()

        for c in range(chunks):
            for dst in range(last):
                xout_copy(c, dst).wait_send()
            pltpu.make_async_copy(xf.at[c], xout_hbm.at[c], xo_loc.at[c]).wait()


def solution(mesh):
    def program(x_init, h_warm, w_lat, w_qkv, w_o, w_up, w_down, w_out, ada_mods, alpha_coef, beta_coef):
        batch, steps = x_init.shape[0], ada_mods.shape[0]
        chunks = batch * TOK // ROWS
        total = steps * chunks
        any_spec = pl.BlockSpec(memory_space=pl.ANY)
        smem = pl.BlockSpec(memory_space=pltpu.SMEM)
        dma = pltpu.SemaphoreType.DMA
        flops = 2 * total * ROWS * D * D * 13
        x_out, h_last = pl.pallas_call(
            functools.partial(kernel, steps, chunks),
            out_shape=(jax.ShapeDtypeStruct((chunks, ROWS, CH), F32), jax.ShapeDtypeStruct((chunks, ROWS, D), BF16)),
            in_specs=[any_spec] * 9 + [smem] * 2,
            out_specs=(any_spec, any_spec),
            scratch_shapes=[
                pltpu.VMEM((CH, D), BF16), pltpu.VMEM((D, D), BF16), pltpu.VMEM((2 * D, D), BF16),
                pltpu.VMEM((D, D), BF16), pltpu.VMEM((D, FF), BF16), pltpu.VMEM((FF, D), BF16),
                pltpu.VMEM((D, CH), BF16), pltpu.VMEM((2, D, D), BF16), pltpu.VMEM((steps, 6, D), F32),
                pltpu.VMEM((total, ROWS, D), BF16), pltpu.VMEM((total, ROWS, CH), BF16),
                pltpu.VMEM((chunks, ROWS, CH), F32), pltpu.VMEM((ROWS, CH), F32),
                pltpu.VMEM((ROWS, D), F32), pltpu.VMEM((ROWS, D), F32),
                pltpu.VMEM((ROWS, D), BF16), pltpu.VMEM((ROWS, D), BF16),
                pltpu.VMEM((ROWS, D), BF16), pltpu.VMEM((2 * D, ROWS), BF16), pltpu.VMEM((ROWS, D), BF16),
                pltpu.VMEM((ROWS, FF), BF16),
                dma((10,)), dma((chunks,)), dma((total - chunks,)), dma((total - chunks,)),
                dma((STAGES - 1, total - chunks)), dma((total - chunks,)),
                dma((STAGES - 1, chunks)), dma((chunks,)), dma((chunks,)), dma((chunks,)),
            ],
            compiler_params=pltpu.CompilerParams(
                collective_id=0, has_side_effects=True, vmem_limit_bytes=67_043_328),
            cost_estimate=pl.CostEstimate(flops=flops, bytes_accessed=40 << 20, transcendentals=0),
        )(x_init.reshape(chunks, ROWS, CH), h_warm.reshape(STAGES - 1, chunks, ROWS, D),
          w_lat[0], w_qkv[0], w_o.reshape(D, D), w_up[0], w_down[0], w_out, ada_mods[:, 0], alpha_coef, beta_coef)
        return x_out.reshape(x_init.shape), h_last.reshape(1, batch, TOK, D)

    return jax.shard_map(program, mesh=mesh,
                         in_specs=(P('data'), P(None, 'data'), P('stage'), P('stage'), P('stage'), P('stage'), P('stage'), P(), P(None, 'stage'), P(), P()),
                         out_specs=(P('data'), P('stage', 'data')), check_vma=False)
```

time: 1030 us -> 353 us (0.34); the launches traced: 1010 us -> 353 us
  matrix products: 471 us -> 0 us
  Pallas kernels: 0 us -> 342 us
  local copies, waits for them, and re-layouts: 211 us -> 10.6 us
  waiting for transfers between devices: 200 us -> 0 us
  other arithmetic: 104 us -> 0 us
  between operations: 14.9 us -> 0.64 us
  starting transfers between devices: 13.5 us -> 0 us
    dot_general x28 -> x0, matrix products: 471 us -> none  [the longest x4 123 us: value_a9(): jnp.einsum('bnd,df->bnf', u_mlp, w_up, preferred_element_type=jnp.float32)]
    pallas_call x0 -> x1, Pallas kernels: none -> 342 us  [program(): pl.pallas_call(functools.partial(kernel, steps, chunks), out_shape=(jax.S...]
    psum x4 -> x0, waiting for transfers between devices: 137 us -> none  [stage_program(): x_cur = lax.psum(x_last, 'stage')]
    reshape x4 -> x0, local copies, waits for them, and re-layouts: 123 us -> none  [value_a9(): qkv_proj = qkv_proj.reshape(batch_size, tokens, 3, num_heads, head_dim)]
    sub x4 -> x0, other arithmetic: 73.8 us -> none  [value_a9(): attn_probs = jax.nn.softmax(scores, axis=-1).astype(jnp.bfloat16)]
    squeeze x4 -> x1, local copies, waits for them, and re-layouts: 69.5 us -> 0.72 us  [program(): ada_mods[:, 0]]
    ppermute x3 -> x0, waiting for transfers between devices: 63.3 us -> none  [stage_program(): stale_in = lax.ppermute(stage_out, 'stage', perm=forward)]
    reduce_sum x8 -> x0, other arithmetic: 27.2 us -> none  [layer_norm(): row_var = jnp.mean(centered * centered, axis=-1, keepdims=True)]
  transfers between devices with their start and end apart: 7 -> 0, of which waited for: 7 -> 0; matrix products, arithmetic and copies ran while one was open for 2% -> 0% of each run, Pallas kernels for 0% -> 0%
where the time goes in v1:
time: 353 us
  Pallas kernels  342 us (97%)
  local copies, waits for them, and re-layouts  10.6 us (3%)
    pallas_call x1, Pallas kernels, program(): pl.pallas_call(functools.partial(kernel, steps, chunks), out_shape=(jax.S...  342 us
    unnamed x4, local copies, waits for them, and re-layouts  9.9 us

profile of v1, /device:TPU:1, one launch (start us, length us, event | category | flops | bytes accessed | tf_op | source)
XLA Modules:
  0.0 352.8 jit_solution(6250155912155344062)
XLA Ops:
  0.6 0.9 copy.18
  1.6 0.7 copy.16.mods_hbm
  2.3 1.7 copy.15.out_hbm
  4.0 341.5 %shard_map.122 = (f32[8,256,64]{2,1,0:T(8,128)}, bf16[8,256,1024]{2,1,0:T(8,128)(2,1)}) custom-call(f32[8,256,64]{2,1,0:T(8,128)} %bitcast.20, bf16[3,8,256,1024]{3,2,1,0:T(8,128)(2,1)} %bitcast.15, bf16[64,1024]{1,0:T(8,128)(2,1)} %bitcast.21, bf16[1024,3072]{1,0:T(8,128)(2,1)} %bitcast.18, bf16[1024,1024]{1,0:T(8,128)(2,1)} %bitcast.19, ...), custom_call_target="tpu_custom_call" | custom-call | flops 223338299392 | bytes 41943040 | tf_op jit(solution)/shard_map/pallas_call | solution.py:331
  345.6 2.3 copy.21
  347.9 4.9 %copy.22 = bf16[1,32,64,1024]{3,2,1,0:T(8,128)(2,1)} copy(bf16[1,32,64,1024]{3,2,1,0:T(8,128)(2,1)} %bitcast.12) | data formatting | bytes 8388608

commit v2 on v1

v2 whole, which is shorter than its diff:
```python
import functools

import jax
import jax.numpy as jnp
from jax import lax
from jax.experimental import pallas as pl
from jax.experimental.pallas import tpu as pltpu
from jax.sharding import PartitionSpec as P

F32, BF16 = jnp.float32, jnp.bfloat16
MESH = pl.DeviceIdType.MESH
D, HEADS, HEAD, TOK, CH, FF = 1024, 16, 64, 64, 64, 4096
ROWS = 256
RB = 16
STAGES = 4
INV_D = 1.0 / D
GC0 = 0.7978845608028654
GC1 = GC0 * 0.044715
LOG2E = 1.4426950408889634
VMEM_LIMIT = 45 << 20


def dot(a, b):
    return jnp.dot(a, b, preferred_element_type=F32)


def dot_t(a, b):
    return lax.dot_general(a, b, (((1,), (1,)), ((), ())), preferred_element_type=F32)


def merge(first, second):
    total_a = sum(w for w, _ in first)
    total_b = sum(w for w, _ in second)
    ia = ib = 0
    done_a = done_b = 0.0
    while ia < len(first) or ib < len(second):
        take_a = ib >= len(second) or (ia < len(first) and done_a / total_a <= done_b / total_b)
        if take_a:
            w, piece = first[ia]
            ia, done_a = ia + 1, done_a + w
        else:
            w, piece = second[ib]
            ib, done_b = ib + 1, done_b + w
        piece()


def wide(ref, rows=slice(None), tiles=None):
    tiles = range(ref.shape[0]) if tiles is None else tiles
    return jnp.concatenate([ref[c, rows, :] for c in tiles], axis=1)


def put(ref, first, rows, value):
    for c in range(value.shape[1] // 128):
        ref[first + c, rows, :] = value[:, c * 128:(c + 1) * 128].astype(BF16)


def kernel(steps, chunks,
           x_hbm, warm_hbm, lat_hbm, qkv_hbm, o_hbm, up_hbm, down_hbm, out_hbm, mods_hbm, alpha, beta,
           xf, buf,
           wlat, wk, wqvt, wo, wup, wdown, wout_t, wout, wtmp, mods_t, mods,
           xb, ebuf,
           h_l, h_a, h_n, h_b, u_a, u_b, k_s, qv_s, o_s, hid,
           q_sem, s_sem, lat_sem, k_sem, o_sem, up_sem, down_sem,
           warm_sem, st_send, st_recv, x_send, x_recv, xo_send, xo_recv):
    st = lax.axis_index('stage')
    last = STAGES - 1
    total = steps * chunks

    def tiled(src, first, dst, sem):
        return [pltpu.make_async_copy(src.at[:, pl.ds(first + c * 128, 128)], dst.at[c], sem.at[c]) for c in range(dst.shape[0])]

    ld_q = [pltpu.make_async_copy(qkv_hbm.at[:, pl.ds(part * 2 * D, D)], wtmp.at[part], q_sem.at[part]) for part in range(2)]
    ld_s = [pltpu.make_async_copy(src, dst, s_sem.at[n])
            for n, (src, dst) in enumerate(((x_hbm, xf), (mods_hbm, mods_t), (out_hbm, wout_t)))]
    ld_lat = tiled(lat_hbm, 0, wlat, lat_sem)
    ld_k = tiled(qkv_hbm, D, wk, k_sem)
    ld_o = tiled(o_hbm, 0, wo, o_sem)
    ld_up = tiled(up_hbm, 0, wup, up_sem)
    ld_down = tiled(down_hbm, 0, wdown, down_sem)
    warm_stage = jnp.maximum(st - 1, 0)

    def warm_copy(c):
        return pltpu.make_async_copy(warm_hbm.at[warm_stage, c], buf.at[c], warm_sem.at[c])

    for ld in ld_q + ld_s + ld_lat:
        ld.start()
    warm_copy(0).start()
    for ld in ld_k + ld_o:
        ld.start()
    warm_copy(1).start()
    for ld in ld_up + ld_down:
        ld.start()
    for c in range(2, chunks):
        warm_copy(c).start()

    barrier = pltpu.get_barrier_semaphore()
    for k in range(1, STAGES):
        pl.semaphore_signal(barrier, inc=1, device_id={'stage': lax.rem(st + k, STAGES)}, device_id_type=MESH)
    pl.semaphore_wait(barrier, STAGES - 1)

    def stale_copy(k):
        nxt = jnp.minimum(st + 1, last)
        return pltpu.make_async_remote_copy(
            src_ref=buf.at[k], dst_ref=buf.at[k + chunks], send_sem=st_send.at[k], recv_sem=st_recv.at[k],
            device_id={'stage': nxt}, device_id_type=MESH)

    def latent_copy(k, dst):
        return pltpu.make_async_remote_copy(
            src_ref=xb.at[k + chunks], dst_ref=xb.at[k + chunks], send_sem=x_send.at[dst, k], recv_sem=x_recv.at[k],
            device_id={'stage': dst}, device_id_type=MESH)

    def xout_copy(c, dst):
        return pltpu.make_async_remote_copy(
            src_ref=xf.at[c], dst_ref=xf.at[c], send_sem=xo_send.at[dst, c], recv_sem=xo_recv.at[c],
            device_id={'stage': dst}, device_id_type=MESH)

    def wait_inputs(k):
        @pl.when(k < chunks)
        def _():
            warm_copy(k).wait()

        @pl.when(jnp.logical_and(k >= chunks, st > 0))
        def _():
            stale_copy(k - chunks).wait_recv()

        @pl.when(jnp.logical_and(k >= chunks, st < last))
        def _():
            latent_copy(k - chunks, 0).wait_recv()

    def send_stage(k):
        @pl.when(jnp.logical_and(k < total - chunks, st < last))
        def _():
            stale_copy(k).start()

    def finish_latent(k):
        step, c = lax.div(k, chunks), lax.rem(k, chunks)

        @pl.when(st == last)
        def _():
            x_new = alpha[step] * xf[c] + beta[step] * ebuf[...]
            xf[c] = x_new

            @pl.when(step < steps - 1)
            def _():
                xb[k + chunks] = x_new.astype(BF16)
                for dst in range(last):
                    latent_copy(k, dst).start()

            @pl.when(step == steps - 1)
            def _():
                for dst in range(last):
                    xout_copy(c, dst).start()

    lane = lax.broadcasted_iota(jnp.int32, (HEAD, 4 * TOK), 1)
    left = lax.rem(lane, 2 * TOK) < TOK
    zero_q = jnp.zeros((HEAD, 2 * TOK), BF16)
    blocks = [slice(r * RB, (r + 1) * RB) for r in range(ROWS // RB)]

    def norm(h, dst, rows, step, scale, shift):
        mean = jnp.sum(h, axis=-1, keepdims=True) * INV_D
        cen = h - mean
        var = jnp.sum(cen * cen, axis=-1, keepdims=True) * INV_D
        put(dst, 0, rows, cen * lax.rsqrt(var + 1e-6) * mods[step, scale:scale + 1, :] + mods[step, shift:shift + 1, :])

    def latent_pieces(k):
        def latent(n):
            h_l[:, n * 256:(n + 1) * 256] = dot(xb[k], wide(wlat, tiles=(2 * n, 2 * n + 1)))
        return [(64, functools.partial(latent, n)) for n in range(4)]

    def norm1_pieces(k):
        step = lax.div(k, chunks)

        def norm1(rows):
            h = jnp.where(st > 0, buf[k, rows, :].astype(F32), 0.0) + h_l[rows, :]
            h_a[rows, :] = h
            norm(h, u_a, rows, step, 1, 0)
        return [(40, functools.partial(norm1, rows)) for rows in blocks]

    def proj_pieces():
        def proj_k(n):
            put(k_s, 2 * n, slice(None), dot(wide(u_a), wide(wk, tiles=(2 * n, 2 * n + 1))))

        def proj_qv(n):
            rows = slice(n * 512, (n + 1) * 512)
            put(qv_s, 0, rows, dot_t(wide(wqvt, rows), wide(u_a)))
        return [(256, functools.partial(proj_k, n)) for n in range(4)] + [(512, functools.partial(proj_qv, n)) for n in range(4)]

    h2 = 2 * TOK

    def attend_pieces():
        groups = [(p, hp) for p in range(ROWS // h2) for hp in range(HEADS // 2)]
        probs = {}

        def scores(g):
            p, hp = groups[g]
            r0, l0 = hp * 2 * HEAD, p * h2
            q0 = qv_s[p, r0:r0 + HEAD, :]
            q1 = qv_s[p, r0 + HEAD:r0 + 2 * HEAD, :]
            rhs = jnp.concatenate([jnp.concatenate([q0, zero_q], axis=1), jnp.concatenate([zero_q, q1], axis=1)], axis=0)
            both = dot(k_s[hp, l0:l0 + h2, :], rhs)
            s = jnp.where(left, both[:TOK], both[TOK:])
            e = jnp.exp2((s - jnp.max(s, axis=0, keepdims=True)) * (HEAD ** -0.5 * LOG2E))
            pr = e * (1.0 / jnp.sum(e, axis=0, keepdims=True))
            probs[g] = (jnp.where(left, pr, 0.0).astype(BF16), jnp.where(left, 0.0, pr).astype(BF16))

        def mix(g):
            p, hp = groups[g]
            r0, l0 = D + hp * 2 * HEAD, p * h2
            p_l, p_r = probs.pop(g)
            rhs = jnp.concatenate([
                jnp.concatenate([p_l[:, :h2], zero_q], axis=1), jnp.concatenate([p_r[:, :h2], zero_q], axis=1),
                jnp.concatenate([zero_q, p_l[:, h2:]], axis=1), jnp.concatenate([zero_q, p_r[:, h2:]], axis=1)], axis=0)
            v = jnp.concatenate([qv_s[p, r0:r0 + HEAD, :], qv_s[p, r0 + HEAD:r0 + 2 * HEAD, :]], axis=1)
            ot = dot(v, rhs)
            ot = jnp.concatenate([ot[:, :h2], ot[:, h2:]], axis=0)
            o_s[hp, l0:l0 + h2, :] = ot.T.astype(BF16)

        pieces = []
        for g in range(len(groups) + 1):
            if g < len(groups):
                pieces.append((75, functools.partial(scores, g)))
            if g > 0:
                pieces.append((75, functools.partial(mix, g - 1)))
        return pieces

    def proj_o_pieces(k):
        step = lax.div(k, chunks)

        def proj_o(n):
            cols = slice(n * 256, (n + 1) * 256)
            h_n[:, cols] = h_a[:, cols] + mods[step, 2:3, cols] * dot(wide(o_s), wide(wo, tiles=(2 * n, 2 * n + 1)))
        return [(256, functools.partial(proj_o, n)) for n in range(4)]

    def norm2_pieces(k):
        step = lax.div(k, chunks)
        return [(40, lambda rows=rows: norm(h_n[rows, :], u_b, rows, step, 4, 3)) for rows in blocks]

    def keep_pieces():
        def keep(rows):
            h_b[rows, :] = h_n[rows, :]
        return [(20, functools.partial(keep, rows)) for rows in blocks]

    def up_pieces():
        def up(n):
            z = dot(wide(u_b), wide(wup, tiles=(2 * n, 2 * n + 1)))
            half = 0.5 * z
            t = jnp.tanh(z * (GC0 + GC1 * (z * z)))
            put(hid, 2 * n, slice(None), half + half * t)
        return [(256, functools.partial(up, n)) for n in range(FF // 256)]

    def down_pieces(k):
        step = lax.div(k, chunks)

        def down(n):
            cols = slice(n * 256, (n + 1) * 256)
            y = dot(wide(hid), wide(wdown, tiles=(2 * n, 2 * n + 1)))
            buf[k, :, cols] = (h_b[:, cols] + mods[step, 5:6, cols] * y).astype(BF16)
        return [(1024, functools.partial(down, n)) for n in range(4)]

    def noise(k):
        ebuf[...] = dot(buf[k], wout[...])

    def run(*lists):
        for pieces in lists:
            for _, piece in pieces:
                piece()

    def norms(second, first):
        out = []
        for n in range(len(blocks)):
            out += second[n:n + 1] + first[n:n + 1]
        return out

    def finish_pieces(k, ahead):
        pieces = proj_o_pieces(k)
        if ahead is None:
            return pieces + norm2_pieces(k)
        return pieces + latent_pieces(ahead) + norms(norm2_pieces(k), norm1_pieces(ahead)) + proj_pieces()

    for ld in ld_q:
        ld.wait()

    @pl.loop(0, D // 128)
    def _(ii):
        sl = pl.ds(pl.multiple_of(ii * 128, 128), 128)
        for part in range(2):
            wqvt[ii, part * D:(part + 1) * D, :] = wtmp[part, sl, :].T

    for ld in ld_s + ld_lat:
        ld.wait()
    for c in range(chunks):
        xb[c] = xf[c].astype(BF16)
    wout[...] = wout_t[...].T
    for step in range(steps):
        for j in range(6):
            row = mods_t[j, step:step + 1, :]
            mods[step, j:j + 1, :] = row + 1.0 if j in (1, 4) else row
    wait_inputs(0)
    run(latent_pieces(0), norm1_pieces(0))
    for ld in ld_k:
        ld.wait()
    run(proj_pieces(), attend_pieces())
    for ld in ld_o:
        ld.wait()
    wait_inputs(1)
    run(finish_pieces(0, 1))
    for ld in ld_up + ld_down:
        ld.wait()

    def body(i, ahead):
        if ahead is not None:
            wait_inputs(ahead)
        noise(jnp.maximum(i - 1, 0))
        merge(attend_pieces() + keep_pieces(), up_pieces())
        merge(finish_pieces(i + 1, ahead), down_pieces(i))
        send_stage(i)

    @pl.loop(0, total - 2)
    def _(i):
        body(i, i + 2)

        @pl.when(i > 0)
        def _():
            finish_latent(i - 1)

    body(total - 2, None)
    finish_latent(total - 3)
    noise(total - 2)
    finish_latent(total - 2)
    run(keep_pieces(), up_pieces(), down_pieces(total - 1))
    noise(total - 1)
    finish_latent(total - 1)

    @pl.when(st < last)
    def _():
        @pl.loop(0, total - chunks)
        def _(k):
            stale_copy(k).wait_send()

        for c in range(chunks):
            xout_copy(c, 0).wait_recv()

    @pl.when(st == last)
    def _():
        @pl.loop(0, total - chunks)
        def _(k):
            for dst in range(last):
                latent_copy(k, dst).wait_send()

        for c in range(chunks):
            for dst in range(last):
                xout_copy(c, dst).wait_send()


def solution(mesh):
    def program(x_init, h_warm, w_lat, w_qkv, w_o, w_up, w_down, w_out, ada_mods, alpha_coef, beta_coef):
        batch, steps = x_init.shape[0], ada_mods.shape[0]
        chunks = batch * TOK // ROWS
        total = steps * chunks
        any_spec = pl.BlockSpec(memory_space=pl.ANY)
        vmem_spec = pl.BlockSpec(memory_space=pltpu.VMEM)
        smem = pl.BlockSpec(memory_space=pltpu.SMEM)
        dma = pltpu.SemaphoreType.DMA
        vb, vf = (lambda *shape: pltpu.VMEM(shape, BF16)), (lambda *shape: pltpu.VMEM(shape, F32))
        flops = 2 * total * ROWS * D * D * 13
        x_out, h_all = pl.pallas_call(
            functools.partial(kernel, steps, chunks),
            out_shape=(pltpu.VMEM((chunks, ROWS, CH), F32), pltpu.VMEM((total, ROWS, D), BF16)),
            in_specs=[any_spec] * 9 + [smem] * 2,
            out_specs=(vmem_spec, vmem_spec),
            scratch_shapes=[
                vb(8, CH, 128), vb(8, D, 128), vb(8, 2 * D, 128), vb(8, D, 128), vb(32, D, 128), vb(8, FF, 128),
                vb(CH, D), vb(D, CH), vb(2, D, D), vf(6, steps, D), vf(steps, 6, D),
                vb(total, ROWS, CH), vf(ROWS, CH),
                vf(ROWS, D), vf(ROWS, D), vf(ROWS, D), vf(ROWS, D),
                vb(8, ROWS, 128), vb(8, ROWS, 128), vb(8, ROWS, 128), vb(2, 2 * D, 128), vb(8, ROWS, 128), vb(32, ROWS, 128),
                dma((2,)), dma((3,)), dma((8,)), dma((8,)), dma((8,)), dma((32,)), dma((8,)),
                dma((chunks,)), dma((total - chunks,)), dma((total - chunks,)),
                dma((STAGES - 1, total - chunks)), dma((total - chunks,)), dma((STAGES - 1, chunks)), dma((chunks,)),
            ],
            compiler_params=pltpu.CompilerParams(
                collective_id=0, has_side_effects=True, vmem_limit_bytes=VMEM_LIMIT),
            cost_estimate=pl.CostEstimate(flops=flops, bytes_accessed=40 << 20, transcendentals=0),
        )(x_init.reshape(chunks, ROWS, CH), h_warm.reshape(STAGES - 1, chunks, ROWS, D),
          w_lat[0], w_qkv[0], w_o.reshape(D, D), w_up[0], w_down[0], w_out.T, ada_mods[:, 0].transpose(1, 0, 2), alpha_coef, beta_coef)
        return x_out.reshape(x_init.shape), h_all[total - chunks:].reshape(1, batch, TOK, D)

    return jax.shard_map(program, mesh=mesh,
                         in_specs=(P('data'), P(None, 'data'), P('stage'), P('stage'), P('stage'), P('stage'), P('stage'), P(), P(None, 'stage'), P(), P()),
                         out_specs=(P('data'), P('stage', 'data')), check_vma=False)
```

time: 353 us -> 303 us (0.86)
  Pallas kernels: 342 us -> 297 us
  local copies, waits for them, and re-layouts: 10.6 us -> 5 us
    pallas_call x1, Pallas kernels: 342 us -> 297 us  [program(): pl.pallas_call(functools.partial(kernel, steps, chunks), out_shape=(pltpu...]
    unnamed x4 -> x2, local copies, waits for them, and re-layouts: 9.9 us -> 2.54 us
where the time goes in v2:
time: 303 us
  Pallas kernels  297 us (98%)
  local copies, waits for them, and re-layouts  5 us (2%)
    pallas_call x1, Pallas kernels, program(): pl.pallas_call(functools.partial(kernel, steps, chunks), out_shape=(pltpu...  297 us

profile of v2, /device:TPU:1, one launch (start us, length us, event | category | flops | bytes accessed | tf_op | source)
XLA Modules:
  0.0 303.0 jit_solution(6577066992897824828)
XLA Ops:
  0.6 1.6 copy.15
  2.2 297.4 %shard_map.122 = (f32[8,256,64]{2,1,0:T(8,128)S(1)}, bf16[32,256,1024]{2,1,0:T(8,128)(2,1)S(1)}) custom-call(f32[8,256,64]{2,1,0:T(8,128)} %bitcast.23, bf16[3,8,256,1024]{3,2,1,0:T(8,128)(2,1)} %bitcast.18, bf16[64,1024]{1,0:T(8,128)(2,1)} %bitcast.24, bf16[1024,3072]{1,0:T(8,128)(2,1)} %bitcast.21, bf16[1024,1024]{1,0:T(8,128)(2,1)} %bitcast.22, ...), custom_call_target="tpu_custom_call" | custom-call | flops 223338299392 | bytes 41943040 | tf_op jit(solution)/shard_map/pallas_call | solution.py:366
  299.6 1.0 copy.17
  300.5 2.5 slice.3

commit v3 on v2

--- a/solution.py
+++ b/solution.py
@@ -59,7 +59,7 @@
            xf, buf,
            wlat, wk, wqvt, wo, wup, wdown, wout_t, wout, wtmp, mods_t, mods,
            xb, ebuf,
-           h_l, h_a, h_n, h_b, u_a, u_b, k_s, qv_s, o_s, hid,
+           h_a, h_n, h_b, u_a, u_b, k_s, qv_s, o_s, hid,
            q_sem, s_sem, lat_sem, k_sem, o_sem, up_sem, down_sem,
            warm_sem, st_send, st_recv, x_send, x_recv, xo_send, xo_recv):
     st = lax.axis_index('stage')
@@ -164,16 +164,16 @@
 
     def latent_pieces(k):
         def latent(n):
-            h_l[:, n * 256:(n + 1) * 256] = dot(xb[k], wide(wlat, tiles=(2 * n, 2 * n + 1)))
+            cols = slice(n * 256, (n + 1) * 256)
+            stale = jnp.where(st > 0, buf[k, :, cols].astype(F32), 0.0)
+            h_a[:, cols] = stale + dot(xb[k], wide(wlat, tiles=(2 * n, 2 * n + 1)))
         return [(64, functools.partial(latent, n)) for n in range(4)]
 
     def norm1_pieces(k):
         step = lax.div(k, chunks)
 
         def norm1(rows):
-            h = jnp.where(st > 0, buf[k, rows, :].astype(F32), 0.0) + h_l[rows, :]
-            h_a[rows, :] = h
-            norm(h, u_a, rows, step, 1, 0)
+            norm(h_a[rows, :], u_a, rows, step, 1, 0)
         return [(40, functools.partial(norm1, rows)) for rows in blocks]
 
     def proj_pieces():
@@ -271,11 +271,16 @@
             out += second[n:n + 1] + first[n:n + 1]
         return out
 
-    def finish_pieces(k, ahead):
-        pieces = proj_o_pieces(k)
+    def finish(k, ahead, down):
+        run(proj_o_pieces(k))
+        if ahead is not None:
+            run(latent_pieces(ahead))
+        run(down[:2])
         if ahead is None:
-            return pieces + norm2_pieces(k)
-        return pieces + latent_pieces(ahead) + norms(norm2_pieces(k), norm1_pieces(ahead)) + proj_pieces()
+            run(norm2_pieces(k), down[2:])
+        else:
+            run(norms(norm2_pieces(k), norm1_pieces(ahead)))
+            merge(proj_pieces(), down[2:]) if down else run(proj_pieces())
 
     for ld in ld_q:
         ld.wait()
@@ -293,7 +298,7 @@
     wout[...] = wout_t[...].T
     for step in range(steps):
         for j in range(6):
-            row = mods_t[j, step:step + 1, :]
+            row = mods_t[step * 6 + j]
             mods[step, j:j + 1, :] = row + 1.0 if j in (1, 4) else row
     wait_inputs(0)
     run(latent_pieces(0), norm1_pieces(0))
@@ -303,16 +308,16 @@
     for ld in ld_o:
         ld.wait()
     wait_inputs(1)
-    run(finish_pieces(0, 1))
+    finish(0, 1, [])
     for ld in ld_up + ld_down:
         ld.wait()
 
     def body(i, ahead):
         if ahead is not None:
             wait_inputs(ahead)
+        merge(attend_pieces() + keep_pieces(), up_pieces())
         noise(jnp.maximum(i - 1, 0))
-        merge(attend_pieces() + keep_pieces(), up_pieces())
-        merge(finish_pieces(i + 1, ahead), down_pieces(i))
+        finish(i + 1, ahead, down_pieces(i))
         send_stage(i)
 
     @pl.loop(0, total - 2)
@@ -370,9 +375,9 @@
             out_specs=(vmem_spec, vmem_spec),
             scratch_shapes=[
                 vb(8, CH, 128), vb(8, D, 128), vb(8, 2 * D, 128), vb(8, D, 128), vb(32, D, 128), vb(8, FF, 128),
-                vb(CH, D), vb(D, CH), vb(2, D, D), vf(6, steps, D), vf(steps, 6, D),
+                vb(CH, D), vb(D, CH), vb(2, D, D), vf(6 * steps, 1, D), vf(steps, 6, D),
                 vb(total, ROWS, CH), vf(ROWS, CH),
-                vf(ROWS, D), vf(ROWS, D), vf(ROWS, D), vf(ROWS, D),
+                vf(ROWS, D), vf(ROWS, D), vf(ROWS, D),
                 vb(8, ROWS, 128), vb(8, ROWS, 128), vb(8, ROWS, 128), vb(2, 2 * D, 128), vb(8, ROWS, 128), vb(32, ROWS, 128),
                 dma((2,)), dma((3,)), dma((8,)), dma((8,)), dma((8,)), dma((32,)), dma((8,)),
                 dma((chunks,)), dma((total - chunks,)), dma((total - chunks,)),
@@ -382,7 +387,7 @@
                 collective_id=0, has_side_effects=True, vmem_limit_bytes=VMEM_LIMIT),
             cost_estimate=pl.CostEstimate(flops=flops, bytes_accessed=40 << 20, transcendentals=0),
         )(x_init.reshape(chunks, ROWS, CH), h_warm.reshape(STAGES - 1, chunks, ROWS, D),
-          w_lat[0], w_qkv[0], w_o.reshape(D, D), w_up[0], w_down[0], w_out.T, ada_mods[:, 0].transpose(1, 0, 2), alpha_coef, beta_coef)
+          w_lat[0], w_qkv[0], w_o.reshape(D, D), w_up[0], w_down[0], w_out.T, ada_mods.reshape(steps * 6, 1, D), alpha_coef, beta_coef)
         return x_out.reshape(x_init.shape), h_all[total - chunks:].reshape(1, batch, TOK, D)
 
     return jax.shard_map(program, mesh=mesh,

time: 303 us -> 290 us (0.957)
  Pallas kernels: 297 us -> 286 us
    pallas_call x1, Pallas kernels: 297 us -> 286 us  [program(): pl.pallas_call(functools.partial(kernel, steps, chunks), out_shape=(pltpu...]
where the time goes in v3:
time: 290 us
  Pallas kernels  286 us (99%)
  local copies, waits for them, and re-layouts  3.43 us (1%)
    pallas_call x1, Pallas kernels, program(): pl.pallas_call(functools.partial(kernel, steps, chunks), out_shape=(pltpu...  286 us

profile of v3, /device:TPU:1, one launch (start us, length us, event | category | flops | bytes accessed | tf_op | source)
XLA Modules:
  0.0 290.4 jit_solution(7455897829494916915)
XLA Ops:
  0.6 286.3 %shard_map.122 = (f32[8,256,64]{2,1,0:T(8,128)S(1)}, bf16[32,256,1024]{2,1,0:T(8,128)(2,1)S(1)}) custom-call(f32[8,256,64]{2,1,0:T(8,128)} %bitcast.18, bf16[3,8,256,1024]{3,2,1,0:T(8,128)(2,1)} %bitcast.13, bf16[64,1024]{1,0:T(8,128)(2,1)} %bitcast.19, bf16[1024,3072]{1,0:T(8,128)(2,1)} %bitcast.16, bf16[1024,1024]{1,0:T(8,128)(2,1)} %bitcast.17, ...), custom_call_target="tpu_custom_call" | custom-call | flops 223338299392 | bytes 41943040 | tf_op jit(solution)/shard_map/pallas_call | solution.py:371
  286.9 1.0 copy.14
  287.9 2.5 slice.3

commit v4 on v3

--- a/solution.py
+++ b/solution.py
@@ -22,10 +22,6 @@
 
 def dot(a, b):
     return jnp.dot(a, b, preferred_element_type=F32)
-
-
-def dot_t(a, b):
-    return lax.dot_general(a, b, (((1,), (1,)), ((), ())), preferred_element_type=F32)
 
 
 def merge(first, second):
@@ -57,10 +53,10 @@
 def kernel(steps, chunks,
            x_hbm, warm_hbm, lat_hbm, qkv_hbm, o_hbm, up_hbm, down_hbm, out_hbm, mods_hbm, alpha, beta,
            xf, buf,
-           wlat, wk, wqvt, wo, wup, wdown, wout_t, wout, wtmp, mods_t, mods,
+           wlat, wq, wk, wv, wo, wup, wdown, wout_t, wout, mods_t, mods,
            xb, ebuf,
            h_a, h_n, h_b, u_a, u_b, k_s, qv_s, o_s, hid,
-           q_sem, s_sem, lat_sem, k_sem, o_sem, up_sem, down_sem,
+           s_sem, lat_sem, q_sem, k_sem, v_sem, o_sem, up_sem, down_sem,
            warm_sem, st_send, st_recv, x_send, x_recv, xo_send, xo_recv):
     st = lax.axis_index('stage')
     last = STAGES - 1
@@ -69,11 +65,10 @@
     def tiled(src, first, dst, sem):
         return [pltpu.make_async_copy(src.at[:, pl.ds(first + c * 128, 128)], dst.at[c], sem.at[c]) for c in range(dst.shape[0])]
 
-    ld_q = [pltpu.make_async_copy(qkv_hbm.at[:, pl.ds(part * 2 * D, D)], wtmp.at[part], q_sem.at[part]) for part in range(2)]
     ld_s = [pltpu.make_async_copy(src, dst, s_sem.at[n])
             for n, (src, dst) in enumerate(((x_hbm, xf), (mods_hbm, mods_t), (out_hbm, wout_t)))]
     ld_lat = tiled(lat_hbm, 0, wlat, lat_sem)
-    ld_k = tiled(qkv_hbm, D, wk, k_sem)
+    ld_qkv = tiled(qkv_hbm, 0, wq, q_sem) + tiled(qkv_hbm, D, wk, k_sem) + tiled(qkv_hbm, 2 * D, wv, v_sem)
     ld_o = tiled(o_hbm, 0, wo, o_sem)
     ld_up = tiled(up_hbm, 0, wup, up_sem)
     ld_down = tiled(down_hbm, 0, wdown, down_sem)
@@ -82,21 +77,16 @@
     def warm_copy(c):
         return pltpu.make_async_copy(warm_hbm.at[warm_stage, c], buf.at[c], warm_sem.at[c])
 
-    for ld in ld_q + ld_s + ld_lat:
+    for ld in ld_s + ld_lat:
         ld.start()
     warm_copy(0).start()
-    for ld in ld_k + ld_o:
+    for ld in ld_qkv + ld_o:
         ld.start()
     warm_copy(1).start()
-    for ld in ld_up + ld_down:
-        ld.start()
-    for c in range(2, chunks):
-        warm_copy(c).start()
 
     barrier = pltpu.get_barrier_semaphore()
     for k in range(1, STAGES):
         pl.semaphore_signal(barrier, inc=1, device_id={'stage': lax.rem(st + k, STAGES)}, device_id_type=MESH)
-    pl.semaphore_wait(barrier, STAGES - 1)
 
     def stale_copy(k):
         nxt = jnp.minimum(st + 1, last)
@@ -181,9 +171,11 @@
             put(k_s, 2 * n, slice(None), dot(wide(u_a), wide(wk, tiles=(2 * n, 2 * n + 1))))
 
         def proj_qv(n):
-            rows = slice(n * 512, (n + 1) * 512)
-            put(qv_s, 0, rows, dot_t(wide(wqvt, rows), wide(u_a)))
-        return [(256, functools.partial(proj_k, n)) for n in range(4)] + [(512, functools.partial(proj_qv, n)) for n in range(4)]
+            part, w = (0, wq) if n < 4 else (D, wv)
+            n = n % 4
+            val = dot(wide(u_a), wide(w, tiles=(2 * n, 2 * n + 1))).astype(BF16).T
+            put(qv_s, 0, slice(part + n * 256, part + (n + 1) * 256), val)
+        return [(256, functools.partial(proj_qv, n)) for n in range(8)] + [(256, functools.partial(proj_k, n)) for n in range(4)]
 
     h2 = 2 * TOK
 
@@ -213,7 +205,7 @@
             v = jnp.concatenate([qv_s[p, r0:r0 + HEAD, :], qv_s[p, r0 + HEAD:r0 + 2 * HEAD, :]], axis=1)
             ot = dot(v, rhs)
             ot = jnp.concatenate([ot[:, :h2], ot[:, h2:]], axis=0)
-            o_s[hp, l0:l0 + h2, :] = ot.T.astype(BF16)
+            o_s[hp, l0:l0 + h2, :] = ot.astype(BF16).T
 
         pieces = []
         for g in range(len(groups) + 1):
@@ -281,15 +273,6 @@
         else:
             run(norms(norm2_pieces(k), norm1_pieces(ahead)))
             merge(proj_pieces(), down[2:]) if down else run(proj_pieces())
-
-    for ld in ld_q:
-        ld.wait()
-
-    @pl.loop(0, D // 128)
-    def _(ii):
-        sl = pl.ds(pl.multiple_of(ii * 128, 128), 128)
-        for part in range(2):
-            wqvt[ii, part * D:(part + 1) * D, :] = wtmp[part, sl, :].T
 
     for ld in ld_s + ld_lat:
         ld.wait()
@@ -302,8 +285,12 @@
             mods[step, j:j + 1, :] = row + 1.0 if j in (1, 4) else row
     wait_inputs(0)
     run(latent_pieces(0), norm1_pieces(0))
-    for ld in ld_k:
+    for ld in ld_qkv:
         ld.wait()
+    for ld in ld_up + ld_down:
+        ld.start()
+    for c in range(2, chunks):
+        warm_copy(c).start()
     run(proj_pieces(), attend_pieces())
     for ld in ld_o:
         ld.wait()
@@ -311,6 +298,7 @@
     finish(0, 1, [])
     for ld in ld_up + ld_down:
         ld.wait()
+    pl.semaphore_wait(barrier, STAGES - 1)
 
     def body(i, ahead):
         if ahead is not None:
@@ -374,12 +362,12 @@
             in_specs=[any_spec] * 9 + [smem] * 2,
             out_specs=(vmem_spec, vmem_spec),
             scratch_shapes=[
-                vb(8, CH, 128), vb(8, D, 128), vb(8, 2 * D, 128), vb(8, D, 128), vb(32, D, 128), vb(8, FF, 128),
-                vb(CH, D), vb(D, CH), vb(2, D, D), vf(6 * steps, 1, D), vf(steps, 6, D),
+                vb(8, CH, 128), vb(8, D, 128), vb(8, D, 128), vb(8, D, 128), vb(8, D, 128), vb(32, D, 128), vb(8, FF, 128),
+                vb(CH, D), vb(D, CH), vf(6 * steps, 1, D), vf(steps, 6, D),
                 vb(total, ROWS, CH), vf(ROWS, CH),
                 vf(ROWS, D), vf(ROWS, D), vf(ROWS, D),
                 vb(8, ROWS, 128), vb(8, ROWS, 128), vb(8, ROWS, 128), vb(2, 2 * D, 128), vb(8, ROWS, 128), vb(32, ROWS, 128),
-                dma((2,)), dma((3,)), dma((8,)), dma((8,)), dma((8,)), dma((32,)), dma((8,)),
+                dma((3,)), dma((8,)), dma((8,)), dma((8,)), dma((8,)), dma((8,)), dma((32,)), dma((8,)),
                 dma((chunks,)), dma((total - chunks,)), dma((total - chunks,)),
                 dma((STAGES - 1, total - chunks)), dma((total - chunks,)), dma((STAGES - 1, chunks)), dma((chunks,)),
             ],

time: 290 us -> 281 us (0.969)
  Pallas kernels: 286 us -> 277 us
    pallas_call x1, Pallas kernels: 286 us -> 277 us  [program(): pl.pallas_call(functools.partial(kernel, steps, chunks), out_shape=(pltpu...]
where the time goes in v4:
time: 281 us
  Pallas kernels  277 us (99%)
  local copies, waits for them, and re-layouts  3.43 us (1%)
    pallas_call x1, Pallas kernels, program(): pl.pallas_call(functools.partial(kernel, steps, chunks), out_shape=(pltpu...  277 us

profile of v4, /device:TPU:1, one launch (start us, length us, event | category | flops | bytes accessed | tf_op | source)
XLA Modules:
  0.0 280.8 jit_solution(1380104216449130475)
XLA Ops:
  0.6 276.7 %shard_map.122 = (f32[8,256,64]{2,1,0:T(8,128)S(1)}, bf16[32,256,1024]{2,1,0:T(8,128)(2,1)S(1)}) custom-call(f32[8,256,64]{2,1,0:T(8,128)} %bitcast.18, bf16[3,8,256,1024]{3,2,1,0:T(8,128)(2,1)} %bitcast.13, bf16[64,1024]{1,0:T(8,128)(2,1)} %bitcast.19, bf16[1024,3072]{1,0:T(8,128)(2,1)} %bitcast.16, bf16[1024,1024]{1,0:T(8,128)(2,1)} %bitcast.17, ...), custom_call_target="tpu_custom_call" | custom-call | flops 223338299392 | bytes 41943040 | tf_op jit(solution)/shard_map/pallas_call | solution.py:359
  277.3 1.0 copy.14
  278.3 2.5 slice.3

commit v5 on v4

--- a/solution.py
+++ b/solution.py
@@ -17,6 +17,7 @@
 GC0 = 0.7978845608028654
 GC1 = GC0 * 0.044715
 LOG2E = 1.4426950408889634
+TRAIL, LAG, LEAD = 3, 4, 3
 VMEM_LIMIT = 45 << 20
 
 
@@ -55,7 +56,7 @@
            xf, buf,
            wlat, wq, wk, wv, wo, wup, wdown, wout_t, wout, mods_t, mods,
            xb, ebuf,
-           h_a, h_n, h_b, u_a, u_b, k_s, qv_s, o_s, hid,
+           h_a, h_n, h_b, u_a, u_b, k_s, qv_s, p_s, o_s, hid,
            s_sem, lat_sem, q_sem, k_sem, v_sem, o_sem, up_sem, down_sem,
            warm_sem, st_send, st_recv, x_send, x_recv, xo_send, xo_recv):
     st = lax.axis_index('stage')
@@ -181,7 +182,6 @@
 
     def attend_pieces():
         groups = [(p, hp) for p in range(ROWS // h2) for hp in range(HEADS // 2)]
-        probs = {}
 
         def scores(g):
             p, hp = groups[g]
@@ -193,27 +193,36 @@
             s = jnp.where(left, both[:TOK], both[TOK:])
             e = jnp.exp2((s - jnp.max(s, axis=0, keepdims=True)) * (HEAD ** -0.5 * LOG2E))
             pr = e * (1.0 / jnp.sum(e, axis=0, keepdims=True))
-            probs[g] = (jnp.where(left, pr, 0.0).astype(BF16), jnp.where(left, 0.0, pr).astype(BF16))
+            put(p_s, 4 * g, slice(None), jnp.where(left, pr, 0.0))
+            put(p_s, 4 * g + 2, slice(None), jnp.where(left, 0.0, pr))
 
         def mix(g):
             p, hp = groups[g]
             r0, l0 = D + hp * 2 * HEAD, p * h2
-            p_l, p_r = probs.pop(g)
             rhs = jnp.concatenate([
-                jnp.concatenate([p_l[:, :h2], zero_q], axis=1), jnp.concatenate([p_r[:, :h2], zero_q], axis=1),
-                jnp.concatenate([zero_q, p_l[:, h2:]], axis=1), jnp.concatenate([zero_q, p_r[:, h2:]], axis=1)], axis=0)
+                jnp.concatenate([p_s[4 * g], zero_q], axis=1), jnp.concatenate([p_s[4 * g + 2], zero_q], axis=1),
+                jnp.concatenate([zero_q, p_s[4 * g + 1]], axis=1), jnp.concatenate([zero_q, p_s[4 * g + 3]], axis=1)], axis=0)
             v = jnp.concatenate([qv_s[p, r0:r0 + HEAD, :], qv_s[p, r0 + HEAD:r0 + 2 * HEAD, :]], axis=1)
             ot = dot(v, rhs)
             ot = jnp.concatenate([ot[:, :h2], ot[:, h2:]], axis=0)
             o_s[hp, l0:l0 + h2, :] = ot.astype(BF16).T
 
-        pieces = []
-        for g in range(len(groups) + 1):
-            if g < len(groups):
-                pieces.append((75, functools.partial(scores, g)))
-            if g > 0:
-                pieces.append((75, functools.partial(mix, g - 1)))
-        return pieces
+        return ([functools.partial(scores, g) for g in range(len(groups))],
+                [functools.partial(mix, g) for g in range(len(groups))])
+
+    def attend_up():
+        scores, mixes = attend_pieces()
+        keeps, ups = keep_pieces(), up_pieces()
+        done_s = done_m = 0
+        for n, (_, up) in enumerate(ups):
+            up()
+            keeps[n][1]()
+            while done_s < min(len(scores), (n + 1) * len(scores) / (len(ups) - TRAIL)):
+                scores[done_s]()
+                done_s += 1
+            while done_m < min(len(mixes), done_s - LAG if n < len(ups) - TRAIL else (n + 1 - LEAD) * len(mixes) / (len(ups) - LEAD)):
+                mixes[done_m]()
+                done_m += 1
 
     def proj_o_pieces(k):
         step = lax.div(k, chunks)
@@ -291,7 +300,10 @@
         ld.start()
     for c in range(2, chunks):
         warm_copy(c).start()
-    run(proj_pieces(), attend_pieces())
+    run(proj_pieces())
+    for pieces in attend_pieces():
+        for piece in pieces:
+            piece()
     for ld in ld_o:
         ld.wait()
     wait_inputs(1)
@@ -303,7 +315,7 @@
     def body(i, ahead):
         if ahead is not None:
             wait_inputs(ahead)
-        merge(attend_pieces() + keep_pieces(), up_pieces())
+        attend_up()
         noise(jnp.maximum(i - 1, 0))
         finish(i + 1, ahead, down_pieces(i))
         send_stage(i)
@@ -366,7 +378,7 @@
                 vb(CH, D), vb(D, CH), vf(6 * steps, 1, D), vf(steps, 6, D),
                 vb(total, ROWS, CH), vf(ROWS, CH),
                 vf(ROWS, D), vf(ROWS, D), vf(ROWS, D),
-                vb(8, ROWS, 128), vb(8, ROWS, 128), vb(8, ROWS, 128), vb(2, 2 * D, 128), vb(8, ROWS, 128), vb(32, ROWS, 128),
+                vb(8, ROWS, 128), vb(8, ROWS, 128), vb(8, ROWS, 128), vb(2, 2 * D, 128), vb(64, TOK, 128), vb(8, ROWS, 128), vb(32, ROWS, 128),
                 dma((3,)), dma((8,)), dma((8,)), dma((8,)), dma((8,)), dma((8,)), dma((32,)), dma((8,)),
                 dma((chunks,)), dma((total - chunks,)), dma((total - chunks,)),
                 dma((STAGES - 1, total - chunks)), dma((total - chunks,)), dma((STAGES - 1, chunks)), dma((chunks,)),

time: 281 us -> 276 us (0.982)
  Pallas kernels: 277 us -> 272 us
    pallas_call x1, Pallas kernels: 277 us -> 272 us  [program(): pl.pallas_call(functools.partial(kernel, steps, chunks), out_shape=(pltpu...]
where the time goes in v5:
time: 276 us
  Pallas kernels  272 us (99%)
  local copies, waits for them, and re-layouts  3.43 us (1%)
    pallas_call x1, Pallas kernels, program(): pl.pallas_call(functools.partial(kernel, steps, chunks), out_shape=(pltpu...  272 us

profile of v5, /device:TPU:1, one launch (start us, length us, event | category | flops | bytes accessed | tf_op | source)
XLA Modules:
  0.0 276.3 jit_solution(12894719880807622197)
XLA Ops:
  0.6 272.2 %shard_map.122 = (f32[8,256,64]{2,1,0:T(8,128)S(1)}, bf16[32,256,1024]{2,1,0:T(8,128)(2,1)S(1)}) custom-call(f32[8,256,64]{2,1,0:T(8,128)} %bitcast.18, bf16[3,8,256,1024]{3,2,1,0:T(8,128)(2,1)} %bitcast.13, bf16[64,1024]{1,0:T(8,128)(2,1)} %bitcast.19, bf16[1024,3072]{1,0:T(8,128)(2,1)} %bitcast.16, bf16[1024,1024]{1,0:T(8,128)(2,1)} %bitcast.17, ...), custom_call_target="tpu_custom_call" | custom-call | flops 223338299392 | bytes 41943040 | tf_op jit(solution)/shard_map/pallas_call | solution.py:371
  272.9 1.0 copy.14
  273.9 2.5 slice.3

commit v6 on v5

--- a/solution.py
+++ b/solution.py
@@ -54,7 +54,7 @@
 def kernel(steps, chunks,
            x_hbm, warm_hbm, lat_hbm, qkv_hbm, o_hbm, up_hbm, down_hbm, out_hbm, mods_hbm, alpha, beta,
            xf, buf,
-           wlat, wq, wk, wv, wo, wup, wdown, wout_t, wout, mods_t, mods,
+           wlat, wq, wk, wv, wo, wup, wdown, wout_t, mods_t, mods,
            xb, ebuf,
            h_a, h_n, h_b, u_a, u_b, k_s, qv_s, p_s, o_s, hid,
            s_sem, lat_sem, q_sem, k_sem, v_sem, o_sem, up_sem, down_sem,
@@ -123,12 +123,12 @@
         def _():
             stale_copy(k).start()
 
-    def finish_latent(k):
+    def finish_latent(k, slot):
         step, c = lax.div(k, chunks), lax.rem(k, chunks)
 
         @pl.when(st == last)
         def _():
-            x_new = alpha[step] * xf[c] + beta[step] * ebuf[...]
+            x_new = alpha[step] * xf[c] + beta[step] * ebuf[slot]
             xf[c] = x_new
 
             @pl.when(step < steps - 1)
@@ -212,11 +212,10 @@
 
     def attend_up():
         scores, mixes = attend_pieces()
-        keeps, ups = keep_pieces(), up_pieces()
+        ups = up_pieces()
         done_s = done_m = 0
         for n, (_, up) in enumerate(ups):
             up()
-            keeps[n][1]()
             while done_s < min(len(scores), (n + 1) * len(scores) / (len(ups) - TRAIL)):
                 scores[done_s]()
                 done_s += 1
@@ -258,8 +257,8 @@
             buf[k, :, cols] = (h_b[:, cols] + mods[step, 5:6, cols] * y).astype(BF16)
         return [(1024, functools.partial(down, n)) for n in range(4)]
 
-    def noise(k):
-        ebuf[...] = dot(buf[k], wout[...])
+    def noise(k, slot):
+        ebuf[slot] = lax.dot_general(wout_t[...], buf[k], (((1,), (1,)), ((), ())), preferred_element_type=F32).T
 
     def run(*lists):
         for pieces in lists:
@@ -287,7 +286,6 @@
         ld.wait()
     for c in range(chunks):
         xb[c] = xf[c].astype(BF16)
-    wout[...] = wout_t[...].T
     for step in range(steps):
         for j in range(6):
             row = mods_t[step * 6 + j]
@@ -308,33 +306,39 @@
         ld.wait()
     wait_inputs(1)
     finish(0, 1, [])
+    run(keep_pieces())
     for ld in ld_up + ld_down:
         ld.wait()
     pl.semaphore_wait(barrier, STAGES - 1)
 
-    def body(i, ahead):
-        if ahead is not None:
-            wait_inputs(ahead)
+    def body(i, ahead, slot):
         attend_up()
-        noise(jnp.maximum(i - 1, 0))
+        noise(jnp.maximum(i - 1, 0), slot)
         finish(i + 1, ahead, down_pieces(i))
+        run(keep_pieces())
+
+    @pl.loop(0, (total - 2) // 2)
+    def _(pair):
+        i = 2 * pair
+        wait_inputs(i + 2)
+        wait_inputs(i + 3)
+        body(i, i + 2, 0)
+        body(i + 1, i + 3, 1)
         send_stage(i)
-
-    @pl.loop(0, total - 2)
-    def _(i):
-        body(i, i + 2)
+        send_stage(i + 1)
 
         @pl.when(i > 0)
         def _():
-            finish_latent(i - 1)
-
-    body(total - 2, None)
-    finish_latent(total - 3)
-    noise(total - 2)
-    finish_latent(total - 2)
-    run(keep_pieces(), up_pieces(), down_pieces(total - 1))
-    noise(total - 1)
-    finish_latent(total - 1)
+            finish_latent(i - 1, 0)
+        finish_latent(i, 1)
+
+    body(total - 2, None, 0)
+    finish_latent(total - 3, 0)
+    noise(total - 2, 1)
+    finish_latent(total - 2, 1)
+    run(up_pieces(), down_pieces(total - 1))
+    noise(total - 1, 0)
+    finish_latent(total - 1, 0)
 
     @pl.when(st < last)
     def _():
@@ -375,8 +379,8 @@
             out_specs=(vmem_spec, vmem_spec),
             scratch_shapes=[
                 vb(8, CH, 128), vb(8, D, 128), vb(8, D, 128), vb(8, D, 128), vb(8, D, 128), vb(32, D, 128), vb(8, FF, 128),
-                vb(CH, D), vb(D, CH), vf(6 * steps, 1, D), vf(steps, 6, D),
-                vb(total, ROWS, CH), vf(ROWS, CH),
+                vb(CH, D), vf(6 * steps, 1, D), vf(steps, 6, D),
+                vb(total, ROWS, CH), vf(2, ROWS, CH),
                 vf(ROWS, D), vf(ROWS, D), vf(ROWS, D),
                 vb(8, ROWS, 128), vb(8, ROWS, 128), vb(8, ROWS, 128), vb(2, 2 * D, 128), vb(64, TOK, 128), vb(8, ROWS, 128), vb(32, ROWS, 128),
                 dma((3,)), dma((8,)), dma((8,)), dma((8,)), dma((8,)), dma((8,)), dma((32,)), dma((8,)),

time: 276 us -> 274 us (level)
  no operation moved by 1% of the time
where the time goes in v6:
time: 274 us
  Pallas kernels  270 us (99%)
  local copies, waits for them, and re-layouts  3.43 us (1%)
    pallas_call x1, Pallas kernels, program(): pl.pallas_call(functools.partial(kernel, steps, chunks), out_shape=(pltpu...  270 us

profile of v6, /device:TPU:1, one launch (start us, length us, event | category | flops | bytes accessed | tf_op | source)
XLA Modules:
  0.0 274.3 jit_solution(16344307486395895793)
XLA Ops:
  0.6 270.3 %shard_map.122 = (f32[8,256,64]{2,1,0:T(8,128)S(1)}, bf16[32,256,1024]{2,1,0:T(8,128)(2,1)S(1)}) custom-call(f32[8,256,64]{2,1,0:T(8,128)} %bitcast.18, bf16[3,8,256,1024]{3,2,1,0:T(8,128)(2,1)} %bitcast.13, bf16[64,1024]{1,0:T(8,128)(2,1)} %bitcast.19, bf16[1024,3072]{1,0:T(8,128)(2,1)} %bitcast.16, bf16[1024,1024]{1,0:T(8,128)(2,1)} %bitcast.17, ...), custom_call_target="tpu_custom_call" | custom-call | flops 223338299392 | bytes 41943040 | tf_op jit(solution)/shard_map/pallas_call | solution.py:375
  270.9 1.0 copy.14
  271.9 2.5 slice.3
